TPU v7x, 32 devices: a whole 2x2x4 slice. The times are simulated.
32 devices in a mesh: groups: 2 (over y), ctx: 4 (over z), head: 4 (over x, core).
Axes of the slice: x: 2, y: 2, z: 4, core: 2. Of those that a mesh axis runs over, the one named last changes fastest.
Arguments:
- queries: bfloat16 [2048, 4096], P(('groups', 'ctx'), 'head'), parts along dimension 0, may hold values from -250 to 250
- rotated_key_rows: bfloat16 [2048, 1024], P(('groups', 'ctx'), 'head'), parts along dimension 0, may hold values from -6 to 6
- value_state_rows: bfloat16 [2048, 1024], P(('groups', 'ctx'), 'head'), parts along dimension 0, may hold values from -6 to 6
- retained_positions: int32 [8, 32], P(('groups', 'ctx')), parts along dimension 0, may hold values from 0 to 255, as said below
- anchor_length: int32 [2], P('groups'), parts along dimension 0, may hold values from 1 to 128
- out_proj: bfloat16 [4096, 4096], P('head'), may hold values from -0.125 to 0.125
Outputs:
- attn_out: bfloat16 [2048, 4096], P(('groups', 'ctx'), 'head'), parts along dimension 0
There are 2 independent parts, one for each index of `groups`. A program takes and returns all parts, laid end to end along the dimension named above; an argument that names none is the same for every part. Nothing has to cross between parts.
Inputs may be any that keep to these rules, and one draw needn't show every extreme that they name: `retained_positions`: each row holds 32 different positions in increasing order.
All inputs are finite; a program needn't handle non-finite values.
Results may differ from a plain program's by a relative error of at most 0.015.
Values may be sent and summed in bfloat16 or wider, within the bound.
No kernel may reach another device: no remote copies, remote signals or barrier semaphores. Data moves between devices by JAX's collectives and lax.ppermute only.
A program may use at most 64 MiB of HBM per device.

v0:
```python
import jax
import jax.numpy as jnp
from jax import lax
from jax.sharding import PartitionSpec as P

HEAD_SIZE = 128
ANCHOR = 128
RETAINED_COUNT = 32


def spread(value, axis, source):
    kept = jnp.where(lax.axis_index(axis) == source, value, 0).astype(value.dtype)
    return lax.psum(kept, axis)


def local(queries, rotated_key_rows, value_state_rows, retained_positions, anchor_length, out_proj):
    tok_rows = queries.shape[0]
    kv_heads = rotated_key_rows.shape[1] // HEAD_SIZE
    queries_per_key_head = queries.shape[1] // rotated_key_rows.shape[1]
    inv_root = HEAD_SIZE ** (-0.5)
    my_host = lax.axis_index("ctx")
    heads_q = queries.reshape(tok_rows, kv_heads, queries_per_key_head, HEAD_SIZE)
    places = jnp.arange(tok_rows, dtype=jnp.int32)

    def absorb(running, key_rows, val_rows, allowed):
        maxima, totals, numerator = running
        key_count = key_rows.shape[0]
        key_heads = key_rows.reshape(key_count, kv_heads, HEAD_SIZE)
        val_heads = val_rows.reshape(key_count, kv_heads, HEAD_SIZE)
        scores = (
            jnp.einsum("tkgd,nkd->kgtn", heads_q, key_heads, preferred_element_type=jnp.float32)
            * inv_root
        )
        scores = jnp.where(allowed, scores, -1e30)
        new_max = jnp.maximum(maxima, jnp.max(scores, axis=-1))
        weights = jnp.where(allowed, jnp.exp(scores - new_max[..., None]), 0.0)
        rescale = jnp.exp(maxima - new_max)
        totals = totals * rescale + jnp.sum(weights, axis=-1)
        numerator = numerator * rescale[..., None] + jnp.einsum(
            "kgtn,nkd->kgtd",
            weights.astype(jnp.bfloat16),
            val_heads,
            preferred_element_type=jnp.float32,
        )
        return (new_max, totals, numerator)

    running = (
        jnp.full((kv_heads, queries_per_key_head, tok_rows), -1e30, jnp.float32),
        jnp.zeros((kv_heads, queries_per_key_head, tok_rows), jnp.float32),
        jnp.zeros((kv_heads, queries_per_key_head, tok_rows, HEAD_SIZE), jnp.float32),
    )
    anchor_keys, anchor_vals = (
        spread(rotated_key_rows[:ANCHOR], "ctx", 0),
        spread(value_state_rows[:ANCHOR], "ctx", 0),
    )
    anchor_ok = ((jnp.arange(ANCHOR, dtype=jnp.int32) < anchor_length[0]) & (my_host > 0))[None, :]
    running = absorb(running, anchor_keys, anchor_vals, anchor_ok)
    kept_keys = rotated_key_rows[retained_positions[0]]
    kept_vals = value_state_rows[retained_positions[0]]
    passing_key_rows, passing_value_rows = (
        lax.all_gather(kept_keys, "ctx", axis=0, tiled=True),
        lax.all_gather(kept_vals, "ctx", axis=0, tiled=True),
    )
    key_total = passing_key_rows.shape[0]
    stride = min(key_total, 1024)
    block_len = min(stride, key_total)
    allowed = ((0 + jnp.arange(block_len, dtype=jnp.int32)) // RETAINED_COUNT < my_host)[None, :]
    running = absorb(running, passing_key_rows, passing_value_rows, allowed)
    local_ok = places[None, :] <= places[:, None]
    running = absorb(running, rotated_key_rows, value_state_rows, local_ok)
    maxima, totals, numerator = running
    attended = (
        (numerator / totals[..., None])
        .transpose(2, 0, 1, 3)
        .reshape(tok_rows, -1)
        .astype(jnp.bfloat16)
    )
    partial_value = jnp.dot(attended, out_proj, preferred_element_type=jnp.float32)
    return lax.psum_scatter(
        partial_value.astype(jnp.bfloat16), "head", scatter_dimension=1, tiled=True
    )


def solution(mesh):
    placed = (
        P(("groups", "ctx"), "head"),
        P(("groups", "ctx"), "head"),
        P(("groups", "ctx"), "head"),
        P(("groups", "ctx"), None),
        P("groups"),
        P("head", None),
    )
    return jax.shard_map(
        local, mesh=mesh, in_specs=placed, out_specs=P(("groups", "ctx"), "head"), check_vma=False
    )
```

profile of v0, /device:TPU:0, one launch (start us, length us, event | category | flops | bytes accessed | tf_op | source)
XLA Modules:
  0.0 95.5 jit_solution(15180239776846359299)
XLA Ops:
  6.5 0.0 copy-start.1
  6.5 0.0 all-reduce.3.cloned.1.call-start
  6.5 0.9 slice.6
  7.4 0.1 copy.45
  7.6 0.7 copy.18
  8.3 1.0 %copy.20 = bf16[256,256]{0,1:T(8,128)(2,1)S(1)} copy(bf16[256,256]{1,0:T(8,128)(2,1)} %param.8) | data formatting | bytes 262144 | tf_op args[2]
  9.3 0.6 slice_select_fusion
  10.0 0.0 all-reduce.3.cloned.1.call-update
  10.0 0.0 reduce-scatter.2.cloned.1.call-start
  10.0 0.7 fusion.46
  10.7 1.5 %gather_fusion.1 = bf16[32,256]{1,0:T(8,128)(2,1)S(1)} fusion(bf16[256,256]{1,0:T(8,128)(2,1)} %param.8, s32[1024]{0:T(1024)S(1)} %pad_clamp_fusion), kind=kCustom, calls=%fused_computation.1 | custom fusion | bytes 32896 | tf_op jit(solution)/shard_map/gather | solution.py:59
  12.2 1.5 %gather_fusion = bf16[32,256]{1,0:T(8,128)(2,1)S(1)} fusion(bf16[256,256]{1,0:T(8,128)(2,1)} %param.7, s32[1024]{0:T(1024)S(1)} %pad_clamp_fusion), kind=kCustom, calls=%fused_computation | custom fusion | bytes 32896 | tf_op jit(solution)/shard_map/gather | solution.py:58
  13.8 0.9 reshape.107
  14.7 15.0 %all-gather = bf16[128,256]{1,0:T(8,128)(2,1)S(1)} all-gather(bf16[32,256]{1,0:T(8,128)(2,1)S(1)} %gather_fusion), channel_id=2, replica_groups=mesh['groups'=2,'ctx'=4,'head'=4] {'ctx'}, dimensions={0}, use_global_device_ids=true | all-gather | bytes 81920 | tf_op jit(solution)/shard_map/all_gather | solution.py:61
  29.7 0.1 copy.22
  29.8 0.0 copy-done.1
  29.8 0.4 reshape.103
  30.2 0.0 copy-start
  30.2 0.4 fusion.56
  30.6 0.4 copy-done
  31.0 1.6 %fusion = (f32[2,4,256]{2,1,0:T(4,128)S(1)}, f32[2,256,256,4]{2,1,3,0:T(8,128)S(1)}) fusion(pred[256,256]{0,1:T(8,128)(4,1)S(1)} %iota_compare_fusion, bf16[256,2,4,128]{3,2,1,0:T(4,128)(2,1)} %copy-done, bf16[256,2,128,1]{2,1,0,3:T(2,128)(2,1)S(1)} %bitcast.125), kind=kOutput, calls=%fused_computation.5 | convolution fusion | flops 135788544 | bytes 2826240 | tf_op jit(solution)/shard_map/tkgd,nkd->kgtn/dot_general | solution.py:31
  32.6 13.3 %all-gather.1 = bf16[128,256]{1,0:T(8,128)(2,1)S(1)} all-gather(bf16[32,256]{1,0:T(8,128)(2,1)S(1)} %gather_fusion.1), channel_id=3, replica_groups=mesh['groups'=2,'ctx'=4,'head'=4] {'ctx'}, dimensions={0}, use_global_device_ids=true | all-gather | bytes 81920 | tf_op jit(solution)/shard_map/all_gather | solution.py:62
  45.8 0.1 copy.25
  46.6 1.1 %all-reduce.3.cloned.1.call-done = (bf16[128,2,128]{2,0,1:T(8,128)(2,1)}, bf16[128,2,128]{0,2,1:T(8,128)(2,1)}) async-done(((bf16[128,2,128]{2,0,1:T(8,128)(2,1)}, bf16[128,2,128]{0,2,1:T(8,128)(2,1)}), (bf16[128,2,128]{2,0,1:T(8,128)(2,1)}, bf16[128,2,128]{0,2,1:T(8,128)(2,1)})) %all-reduce.3.cloned.1.call-update) | async-done | bytes 131088 | tf_op jit(solution)/shard_map/psum | solution.py:13
  47.8 1.4 %fusion.57 = (f32[2,4,256]{2,1,0:T(4,128)S(1)}, f32[2,4,256,128]{2,3,1,0:T(8,128)S(1)}) fusion(bf16[256,2,4,128]{3,2,1,0:T(4,128)(2,1)} %copy-done, bf16[128,2,128]{2,0,1:T(8,128)(2,1)} %get-tuple-element.5, pred[128]{0:T(512)(128)(4,1)S(1)} %compare_and_fusion), kind=kOutput, calls=%fused_computation.82 | convolution fusion | flops 67893248 | bytes 1646720 | tf_op jit(solution)/shard_map/tkgd,nkd->kgtn/dot_general | solution.py:31
  49.2 0.5 fusion.1
  49.7 0.0 copy-start.2
  49.7 0.0 slice-start
  49.7 0.4 convolution_bitcast_fusion
  50.1 0.5 fusion.20
  50.6 0.0 copy-done.2
  50.6 0.4 fusion.8
  51.0 0.0 slice-start.1
  51.0 0.7 fusion.13
  51.7 0.2 slice-done
  51.9 1.5 %slice-done.1 = s8[4194304]{0:T(1024)(128)(4,1)S(1)} async-done(((s8[8388608]{0:T(1024)(128)(4,1)}), s8[4194304]{0:T(1024)(128)(4,1)S(1)}, s32[]{:S(2)}) %slice-start.1) | async-done | bytes 4194328
  53.4 3.7 %convolution_convert_fusion = bf16[256,4096]{1,0:T(8,128)(2,1)} fusion(bf16[256,1024]{0,1:T(8,128)(2,1)S(1)} %bitcast.124, bf16[1024,4096]{1,0:T(8,128)(2,1)S(1)} %bitcast.123), kind=kOutput, calls=%fused_computation.2 | convolution fusion | flops 2148532224 | bytes 11010048 | tf_op jit(solution)/shard_map/dot_general | solution.py:78
  57.2 0.0 reduce-scatter.2.cloned.1.call-update
  57.2 31.5 %reduce-scatter.2.cloned.1.call-done = bf16[256,1024]{1,0:T(8,128)(2,1)} async-done(((bf16[256,4096]{1,0:T(8,128)(2,1)}), bf16[256,1024]{1,0:T(8,128)(2,1)}) %reduce-scatter.2.cloned.1.call-update) | async-done | bytes 524304 | tf_op jit(solution)/shard_map/reduce_scatter | solution.py:79
  (8 shorter events, 0.1 us)
Async XLA Ops:
  6.5 23.3 %copy-start.1 = (bf16[256,1024]{1,0:T(8,128)(2,1)S(1)}, bf16[256,1024]{1,0:T(8,128)(2,1)}, u32[]{:S(2)}) copy-start(bf16[256,1024]{1,0:T(8,128)(2,1)} %param.6) | copy-start | bytes 1572868
  6.5 41.2 %all-reduce.3.cloned.1.call-start = ((), (), s32[]{:S(2)}) async-start(), calls=%async_computation.2 | async-start | bytes 262144 | tf_op jit(solution)/shard_map/psum | solution.py:13
  10.0 78.7 %reduce-scatter.2.cloned.1.call-start = ((), (), s32[]{:S(2)}) async-start(), calls=%async_computation.1 | async-start | bytes 2621440 | tf_op jit(solution)/shard_map/reduce_scatter | solution.py:79
  30.2 0.8 copy-start
  49.7 0.9 copy-start.2
  49.7 2.2 %slice-start = ((s8[8388608]{0:T(1024)(128)(4,1)}), s8[4194304]{0:T(1024)(128)(4,1)S(1)}, s32[]{:S(2)}) async-start(s8[8388608]{0:T(1024)(128)(4,1)} %bitcast.122), calls=%async_computation.3 | async-start | bytes 8388608
  51.0 2.4 %slice-start.1 = ((s8[8388608]{0:T(1024)(128)(4,1)}), s8[4194304]{0:T(1024)(128)(4,1)S(1)}, s32[]{:S(2)}) async-start(s8[8388608]{0:T(1024)(128)(4,1)} %bitcast.122), calls=%async_computation.4 | async-start | bytes 8388608
Sparse Core Ops, SparseCore 0:
  10.1 37.6 all-reduce.2
  57.3 31.3 reduce-scatter.1
where the time goes:
time: 95.8 us; the launch traced here: 95.5 us
  waiting for transfers between devices  32.6 us (34%)
  blocking collectives  28.2 us (29%)
  between operations  14.2 us (15%)
  local copies, waits for them, and re-layouts  9.46 us (10%)
  matrix products  8.54 us (9%)
  other arithmetic  2.37 us (2%)
    reduce_scatter x1, waiting for transfers between devices, local(): lax.psum_scatter(partial_value.astype(jnp.bfloat16), 'head', scatter_dime...  31.5 us
    all_gather x1, blocking collectives, local(): lax.all_gather(kept_keys, 'ctx', axis=0, tiled=True)  15 us
    all_gather x1, blocking collectives, local(): lax.all_gather(kept_vals, 'ctx', axis=0, tiled=True)  13.3 us
    dot_general x1, matrix products, local(): jnp.dot(attended, out_proj, preferred_element_type=jnp.float32)  3.73 us
    dot_general x3, matrix products, absorb(): jnp.einsum('tkgd,nkd->kgtn', heads_q, key_heads, preferred_element_type=j...  3.34 us
    unnamed x12, local copies, waits for them, and re-layouts  3.24 us
  transfers between devices with their start and end apart: 2, of which 2 were waited for; matrix products, arithmetic and copies ran while one was open for 8% of the time, Pallas kernels for 0%

commit v1 on v0

--- a/solution.py
+++ b/solution.py
@@ -1,3 +1,5 @@
+import functools
+
 import jax
 import jax.numpy as jnp
 from jax import lax
@@ -8,12 +10,42 @@
 RETAINED_COUNT = 32
 
 
-def spread(value, axis, source):
-    kept = jnp.where(lax.axis_index(axis) == source, value, 0).astype(value.dtype)
-    return lax.psum(kept, axis)
+def context_rows(keys, values, positions, n):
+    me = lax.axis_index("ctx")
+    first = jnp.concatenate([keys[:ANCHOR], values[:ANCHOR]], axis=1)
+    own = jnp.concatenate([keys, values], axis=1)
+    chosen = (positions[:, None] == jnp.arange(own.shape[0], dtype=jnp.int32)[None, :]).astype(own.dtype)
+    kept = jnp.dot(chosen, own, preferred_element_type=jnp.float32).astype(own.dtype)
+    both = jnp.concatenate([first, kept], axis=0)
+    anchor, passed = 0, []
+    for shift in range(1, n):
+        near = lax.ppermute(both, "ctx", [(0, shift)])
+        rest = [(i, i + shift) for i in range(1, n - shift)]
+        other = lax.ppermute(kept, "ctx", rest) if rest else jnp.zeros_like(kept)
+        anchor = jnp.where(me == shift, near[:ANCHOR], anchor)
+        passed.append(jnp.where(me == shift, near[ANCHOR:], other))
+    return anchor, jnp.concatenate(passed, axis=0)
 
 
-def local(queries, rotated_key_rows, value_state_rows, retained_positions, anchor_length, out_proj):
+def scatter_sum(partial, n):
+    me = lax.axis_index("head")
+    bit = 1
+    width = partial.shape[1] // n
+    held = {0: partial}
+    blocks = {o: lax.dynamic_slice_in_dim(partial, (me ^ o) * width, width, 1) for o in range(n)}
+    while bit < n:
+        pairs = [(i, i ^ bit) for i in range(n)]
+        kept = {}
+        for o in sorted(blocks, reverse=True):
+            if o & bit:
+                got = lax.ppermute(blocks[o].astype(jnp.bfloat16), "head", pairs)
+                kept[o ^ bit] = blocks[o ^ bit].astype(jnp.float32) + got.astype(jnp.float32)
+        blocks = kept
+        bit *= 2
+    return blocks[0].astype(jnp.bfloat16)
+
+
+def local(queries, rotated_key_rows, value_state_rows, retained_positions, anchor_length, out_proj, *, n_ctx, n_head):
     tok_rows = queries.shape[0]
     kv_heads = rotated_key_rows.shape[1] // HEAD_SIZE
     queries_per_key_head = queries.shape[1] // rotated_key_rows.shape[1]
@@ -49,22 +81,13 @@
         jnp.zeros((kv_heads, queries_per_key_head, tok_rows), jnp.float32),
         jnp.zeros((kv_heads, queries_per_key_head, tok_rows, HEAD_SIZE), jnp.float32),
     )
-    anchor_keys, anchor_vals = (
-        spread(rotated_key_rows[:ANCHOR], "ctx", 0),
-        spread(value_state_rows[:ANCHOR], "ctx", 0),
-    )
+    anchor, passed = context_rows(rotated_key_rows, value_state_rows, retained_positions[0], n_ctx)
+    width = rotated_key_rows.shape[1]
+    anchor_keys, anchor_vals = anchor[:, :width], anchor[:, width:]
     anchor_ok = ((jnp.arange(ANCHOR, dtype=jnp.int32) < anchor_length[0]) & (my_host > 0))[None, :]
     running = absorb(running, anchor_keys, anchor_vals, anchor_ok)
-    kept_keys = rotated_key_rows[retained_positions[0]]
-    kept_vals = value_state_rows[retained_positions[0]]
-    passing_key_rows, passing_value_rows = (
-        lax.all_gather(kept_keys, "ctx", axis=0, tiled=True),
-        lax.all_gather(kept_vals, "ctx", axis=0, tiled=True),
-    )
-    key_total = passing_key_rows.shape[0]
-    stride = min(key_total, 1024)
-    block_len = min(stride, key_total)
-    allowed = ((0 + jnp.arange(block_len, dtype=jnp.int32)) // RETAINED_COUNT < my_host)[None, :]
+    passing_key_rows, passing_value_rows = passed[:, :width], passed[:, width:]
+    allowed = (jnp.arange(passed.shape[0], dtype=jnp.int32) // RETAINED_COUNT < my_host)[None, :]
     running = absorb(running, passing_key_rows, passing_value_rows, allowed)
     local_ok = places[None, :] <= places[:, None]
     running = absorb(running, rotated_key_rows, value_state_rows, local_ok)
@@ -76,11 +99,7 @@
         .astype(jnp.bfloat16)
     )
     partial_value = jnp.dot(attended, out_proj, preferred_element_type=jnp.float32)
-    return lax.psum_scatter(
-        partial_value.astype(jnp.bfloat16), "head", scatter_dimension=1, tiled=True
-    )
-
-
+    return scatter_sum(partial_value, n_head)
 def solution(mesh):
     placed = (
         P(("groups", "ctx"), "head"),
@@ -90,6 +109,7 @@
         P("groups"),
         P("head", None),
     )
+    body = functools.partial(local, n_ctx=mesh.shape["ctx"], n_head=mesh.shape["head"])
     return jax.shard_map(
-        local, mesh=mesh, in_specs=placed, out_specs=P(("groups", "ctx"), "head"), check_vma=False
+        body, mesh=mesh, in_specs=placed, out_specs=P(("groups", "ctx"), "head"), check_vma=False
     )

time: 95.8 us -> 51 us (0.53)
  blocking collectives: 28.2 us -> 0 us
  waiting for transfers between devices: 32.6 us -> 14.8 us
  starting transfers between devices: 0.04 us -> 14.2 us
  between operations: 14.2 us -> 0.94 us
  other arithmetic: 2.37 us -> 5.38 us
  matrix products: 8.54 us -> 6.15 us
    reduce_scatter x1 -> x0, waiting for transfers between devices: 31.5 us -> none  [local(): lax.psum_scatter(partial_value.astype(jnp.bfloat16), 'head', scatter_dime...]
    all_gather x2 -> x0, blocking collectives: 28.2 us -> none  [the longest x1 15 us: local(): lax.all_gather(kept_keys, 'ctx', axis=0, tiled=True)]
    ppermute x0 -> x8, waiting for transfers between devices: none -> 14.8 us  [the longest x3 13.9 us: scatter_sum(): got = lax.ppermute(blocks[o].astype(jnp.bfloat16), 'head', pairs)]
    ppermute x0 -> x8, starting transfers between devices: none -> 14.2 us  [the longest x3 10.8 us: context_rows(): near = lax.ppermute(both, 'ctx', [(0, shift)])]
    convert_element_type x0 -> x2, other arithmetic: none -> 3.62 us  [the longest x1 2.26 us: scatter_sum(): return blocks[0].astype(jnp.bfloat16)]
    gather x2 -> x0, local copies, waits for them, and re-layouts: 3.05 us -> none  [the longest x1 1.53 us: local(): kept_keys = rotated_key_rows[retained_positions[0]]]
    dot_general x3, matrix products: 3.34 us -> 1.18 us  [absorb(): jnp.einsum('tkgd,nkd->kgtn', heads_q, key_heads, preferred_element_type=j...]
    dot_general x1, matrix products: 3.73 us -> 2.37 us  [local(): jnp.dot(attended, out_proj, preferred_element_type=jnp.float32)]
  transfers between devices with their start and end apart: 2 -> 8, of which waited for: 2 -> 3; matrix products, arithmetic and copies ran while one was open for 8% -> 15% of each run, Pallas kernels for 0% -> 0%
where the time goes in v1:
time: 51 us; the launch traced here: 50.5 us
  waiting for transfers between devices  14.8 us (29%)
  starting transfers between devices  14.2 us (28%)
  local copies, waits for them, and re-layouts  9.11 us (18%)
  matrix products  6.15 us (12%)
  other arithmetic  5.38 us (11%)
  between operations  0.94 us (2%)
    ppermute x3, waiting for transfers between devices, scatter_sum(): got = lax.ppermute(blocks[o].astype(jnp.bfloat16), 'head', pairs)  13.9 us
    ppermute x3, starting transfers between devices, context_rows(): near = lax.ppermute(both, 'ctx', [(0, shift)])  10.8 us
    unnamed x10, local copies, waits for them, and re-layouts  3.95 us
    dot_general x1, matrix products, local(): jnp.dot(attended, out_proj, preferred_element_type=jnp.float32)  2.37 us
    convert_element_type x1, other arithmetic, scatter_sum(): return blocks[0].astype(jnp.bfloat16)  2.26 us
    ppermute x3, starting transfers between devices, scatter_sum(): got = lax.ppermute(blocks[o].astype(jnp.bfloat16), 'head', pairs)  2.12 us
    slice x2, local copies, waits for them, and re-layouts, context_rows(): first = jnp.concatenate([keys[:ANCHOR], values[:ANCHOR]], axis=1)  1.69 us
    dot_general x3, matrix products, absorb(): jnp.einsum('kgtn,nkd->kgtd', weights.astype(jnp.bfloat16), val_heads, pre...  1.44 us
  transfers between devices with their start and end apart: 8, of which 3 were waited for; matrix products, arithmetic and copies ran while one was open for 15% of the time, Pallas kernels for 0%

profile of v1, /device:TPU:0, one launch (start us, length us, event | category | flops | bytes accessed | tf_op | source)
XLA Modules:
  0.0 50.5 jit_solution(4256628291908577799)
XLA Ops:
  0.0 1.2 %convolution_convert_fusion = bf16[32,512]{1,0:T(8,128)(2,1)S(1)} fusion(bf16[256,256]{1,0:T(8,128)(2,1)} %param.8, bf16[256,256]{1,0:T(8,128)(2,1)} %param.7, s32[32]{0:T(128)} %bitcast.111), kind=kOutput, calls=%fused_computation.21 | convolution fusion | flops 8937472 | bytes 295040 | tf_op jit(solution)/shard_map/dot_general | solution.py:18
  1.2 0.7 %collective-permute-start.4 = (bf16[32,512]{1,0:T(8,128)(2,1)S(1)}, bf16[32,512]{1,0:T(8,128)(2,1)S(1)}, u32[]{:S(2)}, u32[]{:S(2)}) collective-permute-start(bf16[32,512]{1,0:T(8,128)(2,1)S(1)} %convolution_convert_fusion), channel_id=1, source_target_pairs={{4,12},{5,13},{6,14},{7,15},{20,28},{21,29},{22,30},{23,31}} | collective-permute-start | bytes 98312 | tf_op jit(solution)/shard_map/ppermute | solution.py:24
  1.8 0.8 %slice.36 = bf16[128,256]{1,0:T(8,128)(2,1)S(1)} slice(bf16[256,256]{1,0:T(8,128)(2,1)} %param.7), slice={[0:128], [0:256]} | slice | bytes 131072 | tf_op jit(solution)/shard_map/slice | solution.py:15
  2.7 0.8 %slice.37 = bf16[128,256]{1,0:T(8,128)(2,1)S(1)} slice(bf16[256,256]{1,0:T(8,128)(2,1)} %param.8), slice={[0:128], [0:256]} | slice | bytes 131072 | tf_op jit(solution)/shard_map/slice | solution.py:15
  3.5 0.7 %pad_maximum_fusion = bf16[160,512]{1,0:T(8,128)(2,1)} fusion(bf16[32,512]{1,0:T(8,128)(2,1)S(1)} %convolution_convert_fusion, bf16[128,256]{1,0:T(8,128)(2,1)S(1)} %slice.37, bf16[128,256]{1,0:T(8,128)(2,1)S(1)} %slice.36), kind=kLoop, calls=%fused_computation.51 | loop fusion | flops 491520 | bytes 327680 | tf_op jit(solution)/shard_map/concatenate | solution.py:19
  4.2 6.0 %collective-permute-start.1 = (bf16[160,512]{1,0:T(8,128)(2,1)}, bf16[160,512]{1,0:T(8,128)(2,1)S(1)}, u32[]{:S(2)}, u32[]{:S(2)}) collective-permute-start(bf16[160,512]{1,0:T(8,128)(2,1)} %pad_maximum_fusion), channel_id=1, source_target_pairs={{0,8},{1,9},{2,10},{3,11},{16,24},{17,25},{18,26},{19,27}} | collective-permute-start | bytes 491528 | tf_op jit(solution)/shard_map/ppermute | solution.py:22
  10.2 3.5 %collective-permute-start.2 = (bf16[160,512]{1,0:T(8,128)(2,1)}, bf16[160,512]{1,0:T(8,128)(2,1)S(1)}, u32[]{:S(2)}, u32[]{:S(2)}) collective-permute-start(bf16[160,512]{1,0:T(8,128)(2,1)} %pad_maximum_fusion), channel_id=1, source_target_pairs={{0,4},{1,5},{2,6},{3,7},{16,20},{17,21},{18,22},{19,23}} | collective-permute-start | bytes 491528 | tf_op jit(solution)/shard_map/ppermute | solution.py:22
  13.7 0.7 %collective-permute-start.3 = (bf16[32,512]{1,0:T(8,128)(2,1)S(1)}, bf16[32,512]{1,0:T(8,128)(2,1)S(1)}, u32[]{:S(2)}, u32[]{:S(2)}) collective-permute-start(bf16[32,512]{1,0:T(8,128)(2,1)S(1)} %convolution_convert_fusion), channel_id=1, source_target_pairs={{4,8},{8,12},{5,9},{9,13},{6,10},{10,14},{7,11},{11,15},{20,24},{2... | collective-permute-start | bytes 98312 | tf_op jit(solution)/shard_map/ppermute | solution.py:24
  14.3 1.3 %collective-permute-start = (bf16[160,512]{1,0:T(8,128)(2,1)}, bf16[160,512]{1,0:T(8,128)(2,1)S(1)}, u32[]{:S(2)}, u32[]{:S(2)}) collective-permute-start(bf16[160,512]{1,0:T(8,128)(2,1)} %pad_maximum_fusion), channel_id=1, source_target_pairs={{0,12},{1,13},{2,14},{3,15},{16,28},{17,29},{18,30},{19,31}} | collective-permute-start | bytes 491528 | tf_op jit(solution)/shard_map/ppermute | solution.py:22
  15.7 0.0 copy-start.1
  15.7 1.0 %reshape.80 = bf16[256,2,128]{2,1,0:T(2,128)(2,1)S(1)} reshape(bf16[256,256]{1,0:T(8,128)(2,1)} %param.7) | data formatting | bytes 262144 | tf_op jit(solution)/shard_map/reshape | solution.py:60
  16.7 1.4 %reshape.76 = bf16[256,2,4,128]{3,2,1,0:T(4,128)(2,1)S(1)} reshape(bf16[256,1024]{1,0:T(8,128)(2,1)} %param.6) | data formatting | bytes 1048576 | tf_op jit(solution)/shard_map/reshape | solution.py:54
  18.1 0.5 %fusion = (f32[2,4,256]{2,1,0:T(4,128)S(1)}, f32[2,256,256,4]{2,1,3,0:T(8,128)S(1)}) fusion(pred[256,256]{0,1:T(8,128)(4,1)S(1)} %iota_compare_fusion, bf16[256,2,4,128]{3,2,1,0:T(4,128)(2,1)S(1)} %reshape.76, bf16[256,2,128,1]{2,1,0,3:T(2,128)(2,1)S(1)} %bitcast.105), kind=kOutput, calls=%fused_computation.2 | convolution fusion | flops 135788544 | bytes 2826240 | tf_op jit(solution)/shard_map/tkgd,nkd->kgtn/dot_general | solution.py:63
  19.3 0.0 copy-done.1
  19.3 0.7 %copy.35 = bf16[256,256]{0,1:T(8,128)(2,1)} copy(bf16[256,256]{1,0:T(8,128)(2,1)S(1)} %copy-done.1) | data formatting | bytes 262144 | tf_op jit(solution)/shard_map/reshape | solution.py:61
  20.1 0.0 collective-permute-done.4
  20.1 0.0 collective-permute-done.1
  20.1 0.9 %collective-permute-done = bf16[160,512]{1,0:T(8,128)(2,1)S(1)} collective-permute-done((bf16[160,512]{1,0:T(8,128)(2,1)}, bf16[160,512]{1,0:T(8,128)(2,1)S(1)}, u32[]{:S(2)}, u32[]{:S(2)}) %collective-permute-start) | collective-permute-done | bytes 163872 | tf_op jit(solution)/shard_map/ppermute | solution.py:22
  21.0 0.0 collective-permute-done.3
  21.0 0.0 collective-permute-done.2
  21.1 0.1 copy.28
  21.3 0.3 fusion.65
  21.6 0.3 fusion.66
  21.9 0.2 fusion.20
  22.2 0.2 fusion.22
  22.4 0.0 slice-start
  22.4 0.5 %fusion.1 = f32[2,4,256]{2,1,0:T(4,128)S(1)} fusion(f32[2,256,256,4]{2,1,3,0:T(8,128)S(1)} %get-tuple-element.19, f32[2,4,256]{2,1,0:T(4,128)S(1)} %get-tuple-element.7, pred[256,256]{0,1:T(8,128)(4,1)S(1)} %iota_compare_fusion), kind=kLoop, calls=%fused_computation.3 | loop fusion | flops 2619392 | bytes 2179072 | tf_op jit(solution)/shard_map/reduce_sum | solution.py:70
  22.9 0.0 copy-start.2
  22.9 0.4 fusion.8
  23.3 0.4 fusion.6
  23.7 0.4 copy-done.2
  24.1 0.0 slice-start.1
  24.1 0.7 %fusion.11 = bf16[256,2,4,128]{0,3,2,1:T(8,128)(2,1)S(1)} fusion(f32[256,2,4,128]{0,3,2,1:T(8,128)S(1)} %fusion.6, bf16[256,2,128,1]{0,2,3,1:T(8,128)(2,1)S(1)} %bitcast.110, f32[2,256,256,4]{2,1,3,0:T(8,128)S(1)} %get-tuple-element.19, f32[2,4,256]{2,1,0:T(4,128)S(1)} %get-tuple-element.7, pred[256,256]{0,1:T(8,128)(4,1)S(1)} %iota_compare_fusion, ...), kind=kOutput, calls=%fused_computation.17 | convolution fusion | flops 137625600 | bytes 3883008 | tf_op jit(solution)/shard_map/kgtn,nkd->kgtd/dot_general | solution.py:71
  24.8 0.0 slice-done
  24.8 1.6 %slice-done.1 = s8[4194304]{0:T(1024)(128)(4,1)S(1)} async-done(((s8[8388608]{0:T(1024)(128)(4,1)}), s8[4194304]{0:T(1024)(128)(4,1)S(1)}, s32[]{:S(2)}) %slice-start.1) | async-done | bytes 4194328
  26.4 2.4 %fusion.67 = f32[256,4096]{1,0:T(8,128)S(1)} fusion(bf16[256,1024]{0,1:T(8,128)(2,1)S(1)} %bitcast.104, bf16[1024,4096]{1,0:T(8,128)(2,1)S(1)} %bitcast.103), kind=kOutput, calls=%fused_computation.97 | convolution fusion | flops 2147483648 | bytes 13107200 | tf_op jit(solution)/shard_map/dot_general | solution.py:101
  28.8 0.0 copy-start
  28.8 1.9 %copy-done = f32[256,4096]{1,0:T(8,128)} copy-done((f32[256,4096]{1,0:T(8,128)}, f32[256,4096]{1,0:T(8,128)S(1)}, u32[]{:S(2)}) %copy-start) | copy-done | bytes 4194328
  30.7 0.2 dynamic-slice_convert_fusion.1
  30.9 0.1 collective-permute-start.6
  31.0 0.5 collective-permute-start.5
  31.5 1.4 %collective-permute-done.6 = bf16[256,1024]{1,0:T(8,128)(2,1)S(1)} collective-permute-done((bf16[256,1024]{1,0:T(8,128)(2,1)S(1)}, bf16[256,1024]{1,0:T(8,128)(2,1)S(1)}, u32[]{:S(2)}, u32[]{:S(2)}) %collective-permute-start.6) | collective-permute-done | bytes 524320 | tf_op jit(solution)/shard_map/ppermute | solution.py:41
  32.9 1.4 %add_convert_fusion.1 = bf16[256,1024]{1,0:T(8,128)(2,1)S(1)} fusion(bf16[256,1024]{1,0:T(8,128)(2,1)S(1)} %collective-permute-done.6, f32[256,4096]{1,0:T(8,128)} %copy-done, s32[]{:T(128)S(6)} %select_n.109), kind=kLoop, calls=%fused_computation.23 | loop fusion | flops 786432 | bytes 2097156 | tf_op jit(solution)/shard_map/convert_element_type | solution.py:41
  34.3 1.6 %collective-permute-start.7 = (bf16[256,1024]{1,0:T(8,128)(2,1)S(1)}, bf16[256,1024]{1,0:T(8,128)(2,1)S(1)}, u32[]{:S(2)}, u32[]{:S(2)}) collective-permute-start(bf16[256,1024]{1,0:T(8,128)(2,1)S(1)} %add_convert_fusion.1), channel_id=1, source_target_pairs={{0,2},{1,3},{2,0},{3,1},{4,6},{5,7},{6,4},{7,5},{8,10},{9,11},{10,... | collective-permute-start | bytes 1572872 | tf_op jit(solution)/shard_map/ppermute | solution.py:41
  35.8 0.0 collective-permute-done.5
  35.8 12.5 %collective-permute-done.7 = bf16[256,1024]{1,0:T(8,128)(2,1)S(1)} collective-permute-done((bf16[256,1024]{1,0:T(8,128)(2,1)S(1)}, bf16[256,1024]{1,0:T(8,128)(2,1)S(1)}, u32[]{:S(2)}, u32[]{:S(2)}) %collective-permute-start.7) | collective-permute-done | bytes 524320 | tf_op jit(solution)/shard_map/ppermute | solution.py:41
  48.3 2.3 %add_convert_fusion = bf16[256,1024]{1,0:T(8,128)(2,1)} fusion(bf16[256,1024]{1,0:T(8,128)(2,1)S(1)} %collective-permute-done.7, bf16[256,1024]{1,0:T(8,128)(2,1)S(1)} %collective-permute-done.5, f32[256,4096]{1,0:T(8,128)} %copy-done, s32[]{:T(128)S(6)} %select_n.107), kind=kLoop, calls=%fused_computation.22 | loop fusion | flops 1310720 | bytes 2621444 | tf_op jit(solution)/shard_map/convert_element_type | solution.py:45
  (16 shorter events, 0.2 us)
Async XLA Ops:
  1.2 18.9 %collective-permute-start.4 = (bf16[32,512]{1,0:T(8,128)(2,1)S(1)}, bf16[32,512]{1,0:T(8,128)(2,1)S(1)}, u32[]{:S(2)}, u32[]{:S(2)}) collective-permute-start(bf16[32,512]{1,0:T(8,128)(2,1)S(1)} %convolution_convert_fusion), channel_id=1, source_target_pairs={{4,12},{5,13},{6,14},{7,15},{20,28},{21,29},{22,30},{23,31}} | collective-permute-start | bytes 98312 | tf_op jit(solution)/shard_map/ppermute | solution.py:24
  4.2 15.9 %collective-permute-start.1 = (bf16[160,512]{1,0:T(8,128)(2,1)}, bf16[160,512]{1,0:T(8,128)(2,1)S(1)}, u32[]{:S(2)}, u32[]{:S(2)}) collective-permute-start(bf16[160,512]{1,0:T(8,128)(2,1)} %pad_maximum_fusion), channel_id=1, source_target_pairs={{0,8},{1,9},{2,10},{3,11},{16,24},{17,25},{18,26},{19,27}} | collective-permute-start | bytes 491528 | tf_op jit(solution)/shard_map/ppermute | solution.py:22
  10.2 10.8 %collective-permute-start.2 = (bf16[160,512]{1,0:T(8,128)(2,1)}, bf16[160,512]{1,0:T(8,128)(2,1)S(1)}, u32[]{:S(2)}, u32[]{:S(2)}) collective-permute-start(bf16[160,512]{1,0:T(8,128)(2,1)} %pad_maximum_fusion), channel_id=1, source_target_pairs={{0,4},{1,5},{2,6},{3,7},{16,20},{17,21},{18,22},{19,23}} | collective-permute-start | bytes 491528 | tf_op jit(solution)/shard_map/ppermute | solution.py:22
  13.7 7.3 %collective-permute-start.3 = (bf16[32,512]{1,0:T(8,128)(2,1)S(1)}, bf16[32,512]{1,0:T(8,128)(2,1)S(1)}, u32[]{:S(2)}, u32[]{:S(2)}) collective-permute-start(bf16[32,512]{1,0:T(8,128)(2,1)S(1)} %convolution_convert_fusion), channel_id=1, source_target_pairs={{4,8},{8,12},{5,9},{9,13},{6,10},{10,14},{7,11},{11,15},{20,24},{2... | collective-permute-start | bytes 98312 | tf_op jit(solution)/shard_map/ppermute | solution.py:24
  14.3 6.6 %collective-permute-start = (bf16[160,512]{1,0:T(8,128)(2,1)}, bf16[160,512]{1,0:T(8,128)(2,1)S(1)}, u32[]{:S(2)}, u32[]{:S(2)}) collective-permute-start(bf16[160,512]{1,0:T(8,128)(2,1)} %pad_maximum_fusion), channel_id=1, source_target_pairs={{0,12},{1,13},{2,14},{3,15},{16,28},{17,29},{18,30},{19,31}} | collective-permute-start | bytes 491528 | tf_op jit(solution)/shard_map/ppermute | solution.py:22
  15.7 3.6 %copy-start.1 = (bf16[256,256]{1,0:T(8,128)(2,1)S(1)}, bf16[256,256]{1,0:T(8,128)(2,1)}, u32[]{:S(2)}) copy-start(bf16[256,256]{1,0:T(8,128)(2,1)} %param.8) | copy-start | bytes 393220
  22.4 2.5 %slice-start = ((s8[8388608]{0:T(1024)(128)(4,1)}), s8[4194304]{0:T(1024)(128)(4,1)S(1)}, s32[]{:S(2)}) async-start(s8[8388608]{0:T(1024)(128)(4,1)} %bitcast.102), calls=%async_computation | async-start | bytes 8388608
  22.9 1.2 %copy-start.2 = (bf16[256,256]{0,1:T(8,128)(2,1)S(1)}, bf16[256,256]{0,1:T(8,128)(2,1)}, u32[]{:S(2)}) copy-start(bf16[256,256]{0,1:T(8,128)(2,1)} %copy.35) | copy-start | bytes 393220
  24.1 2.3 %slice-start.1 = ((s8[8388608]{0:T(1024)(128)(4,1)}), s8[4194304]{0:T(1024)(128)(4,1)S(1)}, s32[]{:S(2)}) async-start(s8[8388608]{0:T(1024)(128)(4,1)} %bitcast.102), calls=%async_computation.1 | async-start | bytes 8388608
  28.8 1.9 %copy-start = (f32[256,4096]{1,0:T(8,128)}, f32[256,4096]{1,0:T(8,128)S(1)}, u32[]{:S(2)}) copy-start(f32[256,4096]{1,0:T(8,128)S(1)} %fusion.67) | copy-start | bytes 12582916
  30.9 2.0 %collective-permute-start.6 = (bf16[256,1024]{1,0:T(8,128)(2,1)S(1)}, bf16[256,1024]{1,0:T(8,128)(2,1)S(1)}, u32[]{:S(2)}, u32[]{:S(2)}) collective-permute-start(bf16[256,1024]{1,0:T(8,128)(2,1)S(1)} %get-tuple-element.10), channel_id=1, source_target_pairs={{0,1},{1,0},{2,3},{3,2},{4,5},{5,4},{6,7},{7,6},{8,9},{9,8},{10,11... | collective-permute-start | bytes 1572872 | tf_op jit(solution)/shard_map/ppermute | solution.py:41
  31.0 4.8 %collective-permute-start.5 = (bf16[256,1024]{1,0:T(8,128)(2,1)S(1)}, bf16[256,1024]{1,0:T(8,128)(2,1)S(1)}, u32[]{:S(2)}, u32[]{:S(2)}) collective-permute-start(bf16[256,1024]{1,0:T(8,128)(2,1)S(1)} %get-tuple-element.9), channel_id=1, source_target_pairs={{0,1},{1,0},{2,3},{3,2},{4,5},{5,4},{6,7},{7,6},{8,9},{9,8},{10,11... | collective-permute-start | bytes 1572872 | tf_op jit(solution)/shard_map/ppermute | solution.py:41
  34.3 14.0 %collective-permute-start.7 = (bf16[256,1024]{1,0:T(8,128)(2,1)S(1)}, bf16[256,1024]{1,0:T(8,128)(2,1)S(1)}, u32[]{:S(2)}, u32[]{:S(2)}) collective-permute-start(bf16[256,1024]{1,0:T(8,128)(2,1)S(1)} %add_convert_fusion.1), channel_id=1, source_target_pairs={{0,2},{1,3},{2,0},{3,1},{4,6},{5,7},{6,4},{7,5},{8,10},{9,11},{10,... | collective-permute-start | bytes 1572872 | tf_op jit(solution)/shard_map/ppermute | solution.py:41

commit v2 on v1

v2 whole, which is shorter than its diff:
```python
import functools

import jax
import jax.numpy as jnp
from jax import lax
from jax.experimental import pallas as pl
from jax.experimental.pallas import tpu as pltpu
from jax.sharding import PartitionSpec as P

HEAD_SIZE = 128
ANCHOR = 128
RETAINED_COUNT = 32
ROWS = 128
LOG2E = 1.4426950408889634
FACTOR = HEAD_SIZE ** (-0.5) * LOG2E
NEVER = -1e30
F32 = jnp.float32
BF16 = jnp.bfloat16
WHOLE = pl.BlockSpec(memory_space=pltpu.VMEM)
SCALARS = pl.BlockSpec(memory_space=pltpu.SMEM)
IN_PLACE = pl.BlockSpec(memory_space=pltpu.HBM)


def dot_rows(a, b):
    return lax.dot_general(a, b, (((1,), (1,)), ((), ())), preferred_element_type=F32)


def grant(mib):
    return pltpu.CompilerParams(vmem_limit_bytes=mib << 20)


def cost(flops, moved, exps=0):
    return pl.CostEstimate(flops=flops, bytes_accessed=moved, transcendentals=exps)


def start_all(moves, sems):
    copies = [pltpu.make_async_copy(src, dst, sems.at[i]) for i, (src, dst) in enumerate(moves)]
    for c in copies:
        c.start()
    return copies


def prepare_kernel(pos_hbm, k_hbm, v_hbm, out_ref, k_ref, v_ref, pos_ref, sems):
    copies = start_all([(pos_hbm, pos_ref), (k_hbm, k_ref), (v_hbm, v_ref)], sems)
    tokens, width = k_ref.shape
    rows = lax.broadcasted_iota(jnp.int32, (tokens, RETAINED_COUNT), 0)
    copies[0].wait()
    chosen = jnp.where(rows == pos_ref[...], 1.0, 0.0).astype(BF16)
    for at, ref, c in ((0, k_ref, copies[1]), (width, v_ref, copies[2])):
        c.wait()
        out_ref[:ANCHOR, at : at + width] = ref[:ANCHOR]
        kept = lax.dot_general(chosen, ref[...], (((0,), (0,)), ((), ())), preferred_element_type=F32)
        out_ref[ANCHOR:, at : at + width] = kept.astype(BF16)


def local_kernel(info_ref, q_hbm, k_ref, v_ref, w_hbm, num_ref, max_ref, sum_ref, q_ref, *rest):
    *weights, sems = rest
    cols = weights[0].shape[1]
    moves = [(q_hbm, q_ref)]
    for o, ref in enumerate(weights):
        at = pl.multiple_of((info_ref[2] ^ o) * cols, 128)
        moves.append((w_hbm.at[:, pl.ds(at, cols)], ref))
    copies = start_all(moves, sems)
    copies[0].wait()
    tokens = q_ref.shape[0]
    heads = q_ref.shape[1] // HEAD_SIZE
    group = q_ref.shape[1] // k_ref.shape[1]
    lane = lax.broadcasted_iota(jnp.int32, (ROWS, 128), 1)
    for top in range(0, tokens, ROWS):
        keys = top + ROWS
        row = lax.broadcasted_iota(jnp.int32, (ROWS, keys), 0) + top
        col = lax.broadcasted_iota(jnp.int32, (ROWS, keys), 1)
        seen = col <= row
        maxima = jnp.zeros((ROWS, 128), F32)
        totals = jnp.zeros((ROWS, 128), F32)
        for h in range(heads):
            at = h * HEAD_SIZE
            kat = (h // group) * HEAD_SIZE
            s = dot_rows(q_ref[top:keys, at : at + HEAD_SIZE], k_ref[:keys, kat : kat + HEAD_SIZE])
            s = jnp.where(seen, s, NEVER)
            m = jnp.max(s, axis=1, keepdims=True)
            p = jnp.exp2((s - m) * FACTOR)
            z = jnp.sum(p, axis=1, keepdims=True)
            num_ref[top:keys, at : at + HEAD_SIZE] = jnp.dot(
                p.astype(BF16), v_ref[:keys, kat : kat + HEAD_SIZE], preferred_element_type=F32
            )
            maxima = jnp.where(lane == h, m, maxima)
            totals = jnp.where(lane == h, z, totals)
        max_ref[top:keys, :] = maxima
        sum_ref[top:keys, :] = totals
    for c in copies[1:]:
        c.wait()


def multiply(att_ref, w_ref, part_ref):
    for top in range(0, part_ref.shape[0], ROWS):
        rows = slice(top, top + ROWS)
        part = jnp.dot(att_ref[rows, :], w_ref[...], preferred_element_type=F32)
        part_ref[rows, :] = part.astype(BF16)


def remote_kernel(info_ref, q_ref, far_ref, num_ref, max_ref, sum_ref, w_ref, att_ref, part_ref):
    tokens = q_ref.shape[0]
    heads = q_ref.shape[1] // HEAD_SIZE
    count, twice = far_ref.shape
    width = twice // 2
    group = q_ref.shape[1] // width
    index = lax.broadcasted_iota(jnp.int32, (1, count), 1)
    mine = info_ref[0]
    limit = jnp.where(mine > 0, info_ref[1], 0)
    seen = index < jnp.where(index < ANCHOR, limit, ANCHOR + mine * RETAINED_COUNT)
    for top in range(0, tokens, ROWS):
        rows = slice(top, top + ROWS)
        for h in range(heads):
            cols = slice(h * HEAD_SIZE, (h + 1) * HEAD_SIZE)
            kat = (h // group) * HEAD_SIZE
            s = dot_rows(q_ref[rows, cols], far_ref[:, kat : kat + HEAD_SIZE])
            s = jnp.where(seen, s, NEVER)
            before = max_ref[rows, h : h + 1]
            m = jnp.maximum(before, jnp.max(s, axis=1, keepdims=True))
            p = jnp.exp2((s - m) * FACTOR)
            scale = jnp.exp2((before - m) * FACTOR)
            z = sum_ref[rows, h : h + 1] * scale + jnp.sum(p, axis=1, keepdims=True)
            o = jnp.dot(
                p.astype(BF16), far_ref[:, width + kat : width + kat + HEAD_SIZE], preferred_element_type=F32
            )
            o = (num_ref[rows, cols] * scale + o) / z
            att_ref[rows, cols] = o.astype(BF16)
    multiply(att_ref, w_ref, part_ref)


def context_rows(message, n):
    me = lax.axis_index("ctx")
    kept = message[ANCHOR:]
    anchor, passed = 0, []
    for shift in range(1, n):
        last = n - 1 - shift
        pairs = [(0, shift)] + ([(last, n - 1)] if last > 0 else [])
        near = lax.ppermute(message, "ctx", pairs)
        rest = [(i, i + shift) for i in range(1, last)]
        block = near[ANCHOR:]
        if rest:
            other = lax.ppermute(kept, "ctx", rest)
            block = jnp.where((me == shift) | (me == n - 1), block, other)
        anchor = jnp.where(me == shift, near[:ANCHOR], anchor)
        passed.append(block)
    passed.append(jnp.zeros_like(kept))
    return jnp.concatenate([anchor] + passed, axis=0)


def local(queries, keys, values, positions, anchor_length, out_proj, *, n_ctx, n_head):
    tokens, model = queries.shape
    width = keys.shape[1]
    heads = model // HEAD_SIZE
    cols = out_proj.shape[1] // n_head
    depth = out_proj.shape[0]
    my_ctx = lax.axis_index("ctx")
    my_head = lax.axis_index("head")

    info = jnp.stack([my_ctx, anchor_length[0], my_head]).astype(jnp.int32)
    fixed = [pltpu.with_memory_space_constraint(x, pltpu.HBM) for x in (positions, keys, values, queries, out_proj)]
    positions, keys, values, queries, out_proj = fixed
    message, keys, values = pl.pallas_call(
        prepare_kernel,
        out_shape=[
            jax.ShapeDtypeStruct((ANCHOR + RETAINED_COUNT, 2 * width), BF16),
            jax.ShapeDtypeStruct(keys.shape, BF16),
            jax.ShapeDtypeStruct(values.shape, BF16),
        ],
        in_specs=[IN_PLACE] * 3,
        out_specs=[WHOLE] * 3,
        scratch_shapes=[pltpu.VMEM(positions.shape, jnp.int32), pltpu.SemaphoreType.DMA((3,))],
        compiler_params=grant(4),
        cost_estimate=cost(2 * tokens * RETAINED_COUNT * width * 2, tokens * width * 4),
    )(positions, keys, values)
    far = context_rows(message, n_ctx)

    num, maxima, totals, queries, *weights = pl.pallas_call(
        local_kernel,
        out_shape=[
            jax.ShapeDtypeStruct((tokens, model), F32),
            jax.ShapeDtypeStruct((tokens, 128), F32),
            jax.ShapeDtypeStruct((tokens, 128), F32),
            jax.ShapeDtypeStruct((tokens, model), BF16),
        ]
        + [jax.ShapeDtypeStruct((depth, cols), BF16)] * n_head,
        in_specs=[SCALARS, IN_PLACE, WHOLE, WHOLE, IN_PLACE],
        out_specs=[WHOLE] * (4 + n_head),
        scratch_shapes=[pltpu.SemaphoreType.DMA((1 + n_head,))],
        compiler_params=grant(24),
        cost_estimate=cost(4 * tokens * tokens * model, tokens * model * 6, heads * tokens * tokens),
    )(info, queries, keys, values, out_proj)

    part_shape = jax.ShapeDtypeStruct((tokens, cols), BF16)
    count = far.shape[0]
    attended, part = pl.pallas_call(
        remote_kernel,
        out_shape=[jax.ShapeDtypeStruct((tokens, model), BF16), part_shape],
        in_specs=[SCALARS] + [WHOLE] * 6,
        out_specs=[WHOLE] * 2,
        compiler_params=grant(12),
        cost_estimate=cost(
            4 * tokens * count * model + 2 * tokens * depth * cols, depth * cols * 2, heads * tokens * count
        ),
    )(info, queries, far, num, maxima, totals, weights[n_head - 1])

    def project(offset):
        return pl.pallas_call(
            multiply,
            out_shape=part_shape,
            in_specs=[WHOLE, WHOLE],
            out_specs=WHOLE,
            compiler_params=grant(8),
            cost_estimate=cost(2 * tokens * depth * cols, depth * cols * 2),
        )(attended, weights[offset])

    blocks = {o: part if o == n_head - 1 else project(o) for o in range(n_head - 1, -1, -1)}
    bit = 1
    while bit < n_head:
        pairs = [(i, i ^ bit) for i in range(n_head)]
        kept = {}
        for o in sorted(blocks, reverse=True):
            if o & bit:
                got = lax.ppermute(blocks[o], "head", pairs)
                kept[o ^ bit] = (blocks[o ^ bit].astype(F32) + got.astype(F32)).astype(BF16)
        blocks = kept
        bit *= 2
    return blocks[0]


def solution(mesh):
    placed = (
        P(("groups", "ctx"), "head"),
        P(("groups", "ctx"), "head"),
        P(("groups", "ctx"), "head"),
        P(("groups", "ctx"), None),
        P("groups"),
        P("head", None),
    )
    body = functools.partial(local, n_ctx=mesh.shape["ctx"], n_head=mesh.shape["head"])
    return jax.shard_map(
        body, mesh=mesh, in_specs=placed, out_specs=P(("groups", "ctx"), "head"), check_vma=False
    )
```

time: 51 us -> 41.9 us (0.82)
  the two profiles are of different devices: /device:TPU:0 before, /device:TPU:16 now
where the time goes in v2:
time: 41.9 us; the launch traced here: 41.6 us
  waiting for transfers between devices  17.6 us (42%)
  Pallas kernels  12.9 us (31%)
  starting transfers between devices  8.93 us (21%)
  other arithmetic  1.4 us (3%)
  between operations  0.82 us (2%)
    ppermute x3, waiting for transfers between devices, local(): got = lax.ppermute(blocks[o], 'head', pairs)  11.6 us
    ppermute x3, starting transfers between devices, context_rows(): near = lax.ppermute(message, 'ctx', pairs)  5.45 us
    pallas_call x1, Pallas kernels, local(): pl.pallas_call(remote_kernel, out_shape=[jax.ShapeDtypeStruct((tokens, mo...  5.09 us
    ppermute x1, waiting for transfers between devices, context_rows(): other = lax.ppermute(kept, 'ctx', rest)  4.43 us
    pallas_call x1, Pallas kernels, local(): pl.pallas_call(local_kernel, out_shape=[jax.ShapeDtypeStruct((tokens, mod...  4.37 us
    ppermute x3, starting transfers between devices, local(): got = lax.ppermute(blocks[o], 'head', pairs)  2.19 us
    pallas_call x3, Pallas kernels, project(): pl.pallas_call(multiply, out_shape=part_shape, in_specs=[WHOLE, WHOLE], o...  2.17 us
    ppermute x3, waiting for transfers between devices, context_rows(): near = lax.ppermute(message, 'ctx', pairs)  1.51 us
  transfers between devices with their start and end apart: 7, of which 3 were waited for; matrix products, arithmetic and copies ran while one was open for 1% of the time, Pallas kernels for 16%

profile of v2, /device:TPU:16, one launch (start us, length us, event | category | flops | bytes accessed | tf_op | source)
XLA Modules:
  0.0 41.6 jit_solution(11027905324891520033)
XLA Ops:
  0.0 1.3 %shard_map.64 = (bf16[160,512]{1,0:T(8,128)(2,1)S(1)}, bf16[256,256]{1,0:T(8,128)(2,1)S(1)}, bf16[256,256]{1,0:T(8,128)(2,1)S(1)}) custom-call(s32[1,32]{1,0:T(1,128)} %pos_hbm.1, bf16[256,256]{1,0:T(8,128)(2,1)} %k_hbm.1, bf16[256,256]{1,0:T(8,128)(2,1)} %v_hbm.1), custom_call_target="tpu_custom_call" | custom-call | flops 8388608 | bytes 262144 | tf_op jit(solution)/shard_map/pallas_call | solution.py:163
  1.3 3.5 %collective-permute-start.2 = (bf16[160,512]{1,0:T(8,128)(2,1)S(1)}, bf16[160,512]{1,0:T(8,128)(2,1)S(1)}, u32[]{:S(2)}, u32[]{:S(2)}) collective-permute-start(bf16[160,512]{1,0:T(8,128)(2,1)S(1)} %get-tuple-element.21), channel_id=1, source_target_pairs={{0,4},{8,12},{1,5},{9,13},{2,6},{10,14},{3,7},{11,15},{16,20},{24,... | collective-permute-start | bytes 491528 | tf_op jit(solution)/shard_map/ppermute | solution.py:139
  4.8 1.3 %collective-permute-start.1 = (bf16[160,512]{1,0:T(8,128)(2,1)S(1)}, bf16[160,512]{1,0:T(8,128)(2,1)S(1)}, u32[]{:S(2)}, u32[]{:S(2)}) collective-permute-start(bf16[160,512]{1,0:T(8,128)(2,1)S(1)} %get-tuple-element.21), channel_id=1, source_target_pairs={{0,8},{4,12},{1,9},{5,13},{2,10},{6,14},{3,11},{7,15},{16,24},{20,... | collective-permute-start | bytes 491528 | tf_op jit(solution)/shard_map/ppermute | solution.py:139
  6.1 0.7 %collective-permute-start = (bf16[160,512]{1,0:T(8,128)(2,1)S(1)}, bf16[160,512]{1,0:T(8,128)(2,1)S(1)}, u32[]{:S(2)}, u32[]{:S(2)}) collective-permute-start(bf16[160,512]{1,0:T(8,128)(2,1)S(1)} %get-tuple-element.21), channel_id=1, source_target_pairs={{0,12},{1,13},{2,14},{3,15},{16,28},{17,29},{18,30},{19,31}} | collective-permute-start | bytes 491528 | tf_op jit(solution)/shard_map/ppermute | solution.py:139
  6.8 1.3 %collective-permute-start.3 = (bf16[32,512]{1,0:T(8,128)(2,1)S(1)}, bf16[32,512]{1,0:T(8,128)(2,1)S(1)}, u32[]{:S(2)}, u32[]{:S(2)}) collective-permute-start(bf16[32,512]{1,0:T(8,128)(2,1)S(1)} %slice.25), channel_id=1, source_target_pairs={{4,8},{5,9},{6,10},{7,11},{20,24},{21,25},{22,26},{23,27}} | collective-permute-start | bytes 98312 | tf_op jit(solution)/shard_map/ppermute | solution.py:143
  8.7 0.1 pad_add_fusion.info_ref
  8.8 4.4 %shard_map.65 = (f32[256,1024]{1,0:T(8,128)S(1)}, f32[256,128]{1,0:T(8,128)S(1)}, f32[256,128]{1,0:T(8,128)S(1)}, bf16[256,1024]{1,0:T(8,128)(2,1)S(1)}, bf16[10...) custom-call(s32[3]{0:T(128)S(1)} %pad_add_fusion.info_ref, ...), custom_call_target="tpu_custom_call" | custom-call | flops 268435456 | bytes 1572864 | tf_op jit(solution)/shard_map/pallas_call | solution.py:178
  13.2 0.0 collective-permute-done.2
  13.2 1.5 %collective-permute-done.1 = bf16[160,512]{1,0:T(8,128)(2,1)S(1)} collective-permute-done((bf16[160,512]{1,0:T(8,128)(2,1)S(1)}, bf16[160,512]{1,0:T(8,128)(2,1)S(1)}, u32[]{:S(2)}, u32[]{:S(2)}) %collective-permute-start.1) | collective-permute-done | bytes 163872 | tf_op jit(solution)/shard_map/ppermute | solution.py:139
  14.7 0.0 collective-permute-done
  14.7 0.1 fusion.2
  14.8 4.4 %collective-permute-done.3 = bf16[32,512]{1,0:T(8,128)(2,1)S(1)} collective-permute-done((bf16[32,512]{1,0:T(8,128)(2,1)S(1)}, bf16[32,512]{1,0:T(8,128)(2,1)S(1)}, u32[]{:S(2)}, u32[]{:S(2)}) %collective-permute-start.3) | collective-permute-done | bytes 32800 | tf_op jit(solution)/shard_map/ppermute | solution.py:143
  19.3 5.1 %shard_map.66 = (bf16[256,1024]{1,0:T(8,128)(2,1)S(1)}, bf16[256,1024]{1,0:T(8,128)(2,1)S(1)}) custom-call(s32[3]{0:T(128)S(1)} %pad_add_fusion.info_ref, bf16[256,1024]{1,0:T(8,128)(2,1)S(1)} %get-tuple-element.20.q_ref, bf16[256,512]{1,0:T(8,128)(2,1)S(1)} %broadcast_dynamic-update-slice_fusion.far_ref, f32[256,1024]{1,0:T(8,128)S(1)} %get-tuple-element.22.num_ref, ...), custom_call_target="tpu_custom_call" | custom-call | flops 805306368 | bytes 2097152 | tf_op jit(solution)/shard_map/pallas_call | solution.py:196
  24.3 0.1 collective-permute-start.5
  24.4 0.7 %shard_map.68 = bf16[256,1024]{1,0:T(8,128)(2,1)S(1)} custom-call(bf16[256,1024]{1,0:T(8,128)(2,1)S(1)} %get-tuple-element.26.att_ref, bf16[1024,1024]{1,0:T(8,128)(2,1)S(1)} %get-tuple-element.28.w_ref), custom_call_target="tpu_custom_call" | custom-call | flops 536870912 | bytes 2097152 | tf_op jit(solution)/shard_map/pallas_call | solution.py:208
  25.2 0.6 %collective-permute-start.4 = (bf16[256,1024]{1,0:T(8,128)(2,1)S(1)}, bf16[256,1024]{1,0:T(8,128)(2,1)S(1)}, u32[]{:S(2)}, u32[]{:S(2)}) collective-permute-start(bf16[256,1024]{1,0:T(8,128)(2,1)S(1)} %shard_map.68), channel_id=1, source_target_pairs={{0,1},{1,0},{2,3},{3,2},{4,5},{5,4},{6,7},{7,6},{8,9},{9,8},{10,11... | collective-permute-start | bytes 1572872 | tf_op jit(solution)/shard_map/ppermute | solution.py:224
  25.7 0.7 %shard_map.69 = bf16[256,1024]{1,0:T(8,128)(2,1)S(1)} custom-call(bf16[256,1024]{1,0:T(8,128)(2,1)S(1)} %get-tuple-element.26.att_ref, bf16[1024,1024]{1,0:T(8,128)(2,1)S(1)} %get-tuple-element.29.w_ref), custom_call_target="tpu_custom_call" | custom-call | flops 536870912 | bytes 2097152 | tf_op jit(solution)/shard_map/pallas_call | solution.py:208
  26.4 0.0 collective-permute-done.5
  26.5 0.2 add_convert_fusion.1
  26.7 1.6 %collective-permute-start.6 = (bf16[256,1024]{1,0:T(8,128)(2,1)S(1)}, bf16[256,1024]{1,0:T(8,128)(2,1)S(1)}, u32[]{:S(2)}, u32[]{:S(2)}) collective-permute-start(bf16[256,1024]{1,0:T(8,128)(2,1)S(1)} %add_convert_fusion.1), channel_id=1, source_target_pairs={{0,2},{1,3},{2,0},{3,1},{4,6},{5,7},{6,4},{7,5},{8,10},{9,11},{10,... | collective-permute-start | bytes 1572872 | tf_op jit(solution)/shard_map/ppermute | solution.py:224
  28.2 0.7 %shard_map.67 = bf16[256,1024]{1,0:T(8,128)(2,1)S(1)} custom-call(bf16[256,1024]{1,0:T(8,128)(2,1)S(1)} %get-tuple-element.26.att_ref, bf16[1024,1024]{1,0:T(8,128)(2,1)S(1)} %get-tuple-element.27.w_ref), custom_call_target="tpu_custom_call" | custom-call | flops 536870912 | bytes 2097152 | tf_op jit(solution)/shard_map/pallas_call | solution.py:208
  28.9 0.0 collective-permute-done.4
  29.0 11.6 %collective-permute-done.6 = bf16[256,1024]{1,0:T(8,128)(2,1)S(1)} collective-permute-done((bf16[256,1024]{1,0:T(8,128)(2,1)S(1)}, bf16[256,1024]{1,0:T(8,128)(2,1)S(1)}, u32[]{:S(2)}, u32[]{:S(2)}) %collective-permute-start.6) | collective-permute-done | bytes 524320 | tf_op jit(solution)/shard_map/ppermute | solution.py:224
  40.6 1.1 %add_convert_fusion = bf16[256,1024]{1,0:T(8,128)(2,1)} fusion(bf16[256,1024]{1,0:T(8,128)(2,1)S(1)} %collective-permute-done.6, bf16[256,1024]{1,0:T(8,128)(2,1)S(1)} %collective-permute-done.4, bf16[256,1024]{1,0:T(8,128)(2,1)S(1)} %shard_map.67), kind=kLoop, calls=%fused_computation | loop fusion | flops 2097152 | bytes 2097152 | tf_op jit(solution)/shard_map/convert_element_type | solution.py:225
  (5 shorter events, 0.0 us)
Async XLA Ops:
  1.3 11.9 %collective-permute-start.2 = (bf16[160,512]{1,0:T(8,128)(2,1)S(1)}, bf16[160,512]{1,0:T(8,128)(2,1)S(1)}, u32[]{:S(2)}, u32[]{:S(2)}) collective-permute-start(bf16[160,512]{1,0:T(8,128)(2,1)S(1)} %get-tuple-element.21), channel_id=1, source_target_pairs={{0,4},{8,12},{1,5},{9,13},{2,6},{10,14},{3,7},{11,15},{16,20},{24,... | collective-permute-start | bytes 491528 | tf_op jit(solution)/shard_map/ppermute | solution.py:139
  4.8 9.9 %collective-permute-start.1 = (bf16[160,512]{1,0:T(8,128)(2,1)S(1)}, bf16[160,512]{1,0:T(8,128)(2,1)S(1)}, u32[]{:S(2)}, u32[]{:S(2)}) collective-permute-start(bf16[160,512]{1,0:T(8,128)(2,1)S(1)} %get-tuple-element.21), channel_id=1, source_target_pairs={{0,8},{4,12},{1,9},{5,13},{2,10},{6,14},{3,11},{7,15},{16,24},{20,... | collective-permute-start | bytes 491528 | tf_op jit(solution)/shard_map/ppermute | solution.py:139
  6.1 8.6 %collective-permute-start = (bf16[160,512]{1,0:T(8,128)(2,1)S(1)}, bf16[160,512]{1,0:T(8,128)(2,1)S(1)}, u32[]{:S(2)}, u32[]{:S(2)}) collective-permute-start(bf16[160,512]{1,0:T(8,128)(2,1)S(1)} %get-tuple-element.21), channel_id=1, source_target_pairs={{0,12},{1,13},{2,14},{3,15},{16,28},{17,29},{18,30},{19,31}} | collective-permute-start | bytes 491528 | tf_op jit(solution)/shard_map/ppermute | solution.py:139
  6.8 12.4 %collective-permute-start.3 = (bf16[32,512]{1,0:T(8,128)(2,1)S(1)}, bf16[32,512]{1,0:T(8,128)(2,1)S(1)}, u32[]{:S(2)}, u32[]{:S(2)}) collective-permute-start(bf16[32,512]{1,0:T(8,128)(2,1)S(1)} %slice.25), channel_id=1, source_target_pairs={{4,8},{5,9},{6,10},{7,11},{20,24},{21,25},{22,26},{23,27}} | collective-permute-start | bytes 98312 | tf_op jit(solution)/shard_map/ppermute | solution.py:143
  24.3 2.1 %collective-permute-start.5 = (bf16[256,1024]{1,0:T(8,128)(2,1)S(1)}, bf16[256,1024]{1,0:T(8,128)(2,1)S(1)}, u32[]{:S(2)}, u32[]{:S(2)}) collective-permute-start(bf16[256,1024]{1,0:T(8,128)(2,1)S(1)} %get-tuple-element.30), channel_id=1, source_target_pairs={{0,1},{1,0},{2,3},{3,2},{4,5},{5,4},{6,7},{7,6},{8,9},{9,8},{10,11... | collective-permute-start | bytes 1572872 | tf_op jit(solution)/shard_map/ppermute | solution.py:224
  25.2 3.8 %collective-permute-start.4 = (bf16[256,1024]{1,0:T(8,128)(2,1)S(1)}, bf16[256,1024]{1,0:T(8,128)(2,1)S(1)}, u32[]{:S(2)}, u32[]{:S(2)}) collective-permute-start(bf16[256,1024]{1,0:T(8,128)(2,1)S(1)} %shard_map.68), channel_id=1, source_target_pairs={{0,1},{1,0},{2,3},{3,2},{4,5},{5,4},{6,7},{7,6},{8,9},{9,8},{10,11... | collective-permute-start | bytes 1572872 | tf_op jit(solution)/shard_map/ppermute | solution.py:224
  26.7 13.9 %collective-permute-start.6 = (bf16[256,1024]{1,0:T(8,128)(2,1)S(1)}, bf16[256,1024]{1,0:T(8,128)(2,1)S(1)}, u32[]{:S(2)}, u32[]{:S(2)}) collective-permute-start(bf16[256,1024]{1,0:T(8,128)(2,1)S(1)} %add_convert_fusion.1), channel_id=1, source_target_pairs={{0,2},{1,3},{2,0},{3,1},{4,6},{5,7},{6,4},{7,5},{8,10},{9,11},{10,... | collective-permute-start | bytes 1572872 | tf_op jit(solution)/shard_map/ppermute | solution.py:224

commit v3 on v2

v3 whole, which is shorter than its diff:
```python
import functools

import jax
import jax.numpy as jnp
from jax import lax
from jax.experimental import pallas as pl
from jax.experimental.pallas import tpu as pltpu
from jax.sharding import PartitionSpec as P


HEAD_SIZE = 128
ANCHOR = 128
RETAINED_COUNT = 32
ROWS = 128
CHUNKS = 2
LOG2E = 1.4426950408889634
FACTOR = HEAD_SIZE ** (-0.5) * LOG2E
NEVER = -1e30
F32 = jnp.float32
BF16 = jnp.bfloat16
WHOLE = pl.BlockSpec(memory_space=pltpu.VMEM)
SCALARS = pl.BlockSpec(memory_space=pltpu.SMEM)
IN_PLACE = pl.BlockSpec(memory_space=pltpu.HBM)


def dot_rows(a, b):
    return lax.dot_general(a, b, (((1,), (1,)), ((), ())), preferred_element_type=F32)


def grant(mib):
    return pltpu.CompilerParams(vmem_limit_bytes=mib << 20)


def cost(flops, moved, exps=0):
    return pl.CostEstimate(flops=flops, bytes_accessed=moved, transcendentals=exps)


def start_all(moves, sems):
    copies = [pltpu.make_async_copy(src, dst, sems.at[i]) for i, (src, dst) in enumerate(moves)]
    for c in copies:
        c.start()
    return copies


def prepare_kernel(pos_hbm, k_hbm, v_hbm, out_ref, k_ref, v_ref, pos_ref, sems):
    copies = start_all([(pos_hbm, pos_ref), (k_hbm, k_ref), (v_hbm, v_ref)], sems)
    tokens, width = k_ref.shape
    rows = lax.broadcasted_iota(jnp.int32, (tokens, RETAINED_COUNT), 0)
    copies[0].wait()
    chosen = jnp.where(rows == pos_ref[...], 1.0, 0.0).astype(BF16)
    for at, ref, c in ((0, k_ref, copies[1]), (width, v_ref, copies[2])):
        c.wait()
        out_ref[:ANCHOR, at : at + width] = ref[:ANCHOR]
        kept = lax.dot_general(chosen, ref[...], (((0,), (0,)), ((), ())), preferred_element_type=F32)
        out_ref[ANCHOR:, at : at + width] = kept.astype(BF16)


def tile(x, t):
    return x[:, t * HEAD_SIZE : (t + 1) * HEAD_SIZE]


def weigh(s, m):
    parts = [jnp.exp2((tile(s, t) - m) * FACTOR) for t in range(s.shape[1] // HEAD_SIZE)]
    return jnp.concatenate(parts, axis=1).astype(BF16)


def with_ones(v):
    return jnp.concatenate([v, jnp.ones_like(v)], axis=1)


def local_kernel(info_ref, q_hbm, k_ref, v_ref, w_hbm, num_ref, max_ref, sum_ref, q_ref, *rest):
    *weights, s_ref, p_ref, sems = rest
    cols = weights[0].shape[1]
    moves = [(q_hbm, q_ref)]
    for o, ref in enumerate(weights):
        at = pl.multiple_of((info_ref[2] ^ o) * cols, 128)
        moves.append((w_hbm.at[:, pl.ds(at, cols)], ref))
    copies = start_all(moves, sems)
    copies[0].wait()
    tokens = q_ref.shape[0]
    heads = q_ref.shape[1] // HEAD_SIZE
    group = q_ref.shape[1] // k_ref.shape[1]
    for top in range(0, tokens, ROWS):
        rows, keys = slice(top, top + ROWS), top + ROWS
        row = lax.broadcasted_iota(jnp.int32, (ROWS, keys), 0) + top
        col = lax.broadcasted_iota(jnp.int32, (ROWS, keys), 1)
        seen = col <= row
        for h in range(heads):
            s = dot_rows(tile(q_ref[rows, :], h), tile(k_ref[:keys, :], h // group))
            s_ref[h, :, :keys] = jnp.where(seen, s, NEVER)
        for h in range(heads):
            s = s_ref[h, :, :keys]
            m = jnp.broadcast_to(jnp.max(s, axis=1, keepdims=True), (ROWS, HEAD_SIZE))
            max_ref[rows, h * HEAD_SIZE : (h + 1) * HEAD_SIZE] = m
            p_ref[h, :, :keys] = weigh(s, m)
        for h in range(heads):
            at = slice(h * HEAD_SIZE, (h + 1) * HEAD_SIZE)
            both = jnp.dot(
                p_ref[h, :, :keys], with_ones(tile(v_ref[:keys, :], h // group)), preferred_element_type=F32
            )
            num_ref[rows, at] = tile(both, 0)
            sum_ref[rows, at] = tile(both, 1)
    for c in copies[1:]:
        c.wait()


def multiply(*refs):
    *att_refs, w_ref, part_ref = refs
    at = 0
    for att_ref in att_refs:
        for top in range(0, att_ref.shape[0], ROWS):
            part = jnp.dot(att_ref[top : top + ROWS, :], w_ref[...], preferred_element_type=F32)
            part_ref[at : at + ROWS, :] = part.astype(BF16)
            at += ROWS


def remote_kernel(
    start, info_ref, q_ref, far_ref, num_ref, max_ref, sum_ref, w_ref, att_ref, part_ref, s_ref, p_ref, m_ref
):
    heads = q_ref.shape[1] // HEAD_SIZE
    count, twice = far_ref.shape
    width = twice // 2
    group = q_ref.shape[1] // width
    index = lax.broadcasted_iota(jnp.int32, (1, count), 1)
    mine = info_ref[0]
    limit = jnp.where(mine > 0, info_ref[1], 0)
    seen = index < jnp.where(index < ANCHOR, limit, ANCHOR + mine * RETAINED_COUNT)
    for top in range(0, att_ref.shape[0], ROWS):
        rows, put = slice(start + top, start + top + ROWS), slice(top, top + ROWS)
        for h in range(heads):
            s = dot_rows(tile(q_ref[rows, :], h), tile(far_ref, h // group))
            s_ref[h] = jnp.where(seen, s, NEVER)
        for h in range(heads):
            at = slice(h * HEAD_SIZE, (h + 1) * HEAD_SIZE)
            s = s_ref[h]
            before = max_ref[rows, at]
            m = jnp.maximum(before, jnp.max(s, axis=1, keepdims=True))
            p_ref[h] = weigh(s, m)
            m_ref[:, at] = jnp.exp2((before - m) * FACTOR)
        for h in range(heads):
            at = slice(h * HEAD_SIZE, (h + 1) * HEAD_SIZE)
            both = jnp.dot(
                p_ref[h], with_ones(tile(far_ref, width // HEAD_SIZE + h // group)), preferred_element_type=F32
            )
            scale = m_ref[:, at]
            o = num_ref[rows, at] * scale + tile(both, 0)
            z = sum_ref[rows, at] * scale + tile(both, 1)
            att_ref[put, at] = (o / z).astype(BF16)
    multiply(att_ref, w_ref, part_ref)


def context_rows(message, n):
    me = lax.axis_index("ctx")
    near = [lax.ppermute(message, "ctx", [(0, shift)]) for shift in range(1, n)]
    kept = message[ANCHOR:]
    anchor, passed = 0, []
    for shift in range(1, n):
        first = near[shift - 1]
        block = first[ANCHOR:]
        rest = [(i, i + shift) for i in range(1, n - shift)]
        if rest:
            other = lax.ppermute(kept, "ctx", rest)
            block = jnp.where(me == shift, block, other)
        anchor = jnp.where(me == shift, first[:ANCHOR], anchor)
        passed.append(block)
    short = -(n - 1) * RETAINED_COUNT % HEAD_SIZE
    passed.append(jnp.zeros((short, kept.shape[1]), kept.dtype))
    return jnp.concatenate([anchor] + passed, axis=0)


def local(*args, n_ctx, n_head):
    return layer(*args, n_ctx, n_head)


def layer(queries, keys, values, positions, anchor_length, out_proj, n_ctx, n_head):
    tokens, model = queries.shape
    width = keys.shape[1]
    heads = model // HEAD_SIZE
    cols = out_proj.shape[1] // n_head
    depth = out_proj.shape[0]
    my_ctx = lax.axis_index("ctx")
    my_head = lax.axis_index("head")

    info = jnp.stack([my_ctx, anchor_length[0], my_head]).astype(jnp.int32)
    fixed = [pltpu.with_memory_space_constraint(x, pltpu.HBM) for x in (positions, keys, values, queries, out_proj)]
    positions, keys, values, queries, out_proj = fixed
    message, keys, values = pl.pallas_call(
        prepare_kernel,
        out_shape=[
            jax.ShapeDtypeStruct((ANCHOR + RETAINED_COUNT, 2 * width), BF16),
            jax.ShapeDtypeStruct(keys.shape, BF16),
            jax.ShapeDtypeStruct(values.shape, BF16),
        ],
        in_specs=[IN_PLACE] * 3,
        out_specs=[WHOLE] * 3,
        scratch_shapes=[pltpu.VMEM(positions.shape, jnp.int32), pltpu.SemaphoreType.DMA((3,))],
        compiler_params=grant(4),
        cost_estimate=cost(2 * tokens * RETAINED_COUNT * width * 2, tokens * width * 4),
    )(positions, keys, values)
    far = context_rows(message, n_ctx)

    num, maxima, totals, queries, *weights = pl.pallas_call(
        local_kernel,
        out_shape=[
            jax.ShapeDtypeStruct((tokens, model), F32),
            jax.ShapeDtypeStruct((tokens, model), F32),
            jax.ShapeDtypeStruct((tokens, model), F32),
            jax.ShapeDtypeStruct((tokens, model), BF16),
        ]
        + [jax.ShapeDtypeStruct((depth, cols), BF16)] * n_head,
        in_specs=[SCALARS, IN_PLACE, WHOLE, WHOLE, IN_PLACE],
        out_specs=[WHOLE] * (4 + n_head),
        scratch_shapes=[
            pltpu.VMEM((heads, ROWS, tokens), F32),
            pltpu.VMEM((heads, ROWS, tokens), BF16),
            pltpu.SemaphoreType.DMA((1 + n_head,)),
        ],
        compiler_params=grant(24),
        cost_estimate=cost(4 * tokens * tokens * model, tokens * model * 6, heads * tokens * tokens),
    )(info, queries, keys, values, out_proj)

    rows = tokens // CHUNKS
    count = far.shape[0]
    half = n_head // 2

    def attend(start, far):
        return pl.pallas_call(
            functools.partial(remote_kernel, start),
            out_shape=[jax.ShapeDtypeStruct((rows, model), BF16), jax.ShapeDtypeStruct((rows, cols), BF16)],
            in_specs=[SCALARS] + [WHOLE] * 6,
            out_specs=[WHOLE] * 2,
            scratch_shapes=[
                pltpu.VMEM((heads, ROWS, count), F32),
                pltpu.VMEM((heads, ROWS, count), BF16),
                pltpu.VMEM((ROWS, model), F32),
            ],
            compiler_params=grant(16),
            cost_estimate=cost(
                4 * rows * count * model + 2 * rows * depth * cols, depth * cols * 2, heads * rows * count
            ),
        )(info, queries, far, num, maxima, totals, weights[n_head - 1])

    def project(attended, offset):
        height = sum(a.shape[0] for a in attended)
        return pl.pallas_call(
            multiply,
            out_shape=jax.ShapeDtypeStruct((height, cols), BF16),
            in_specs=[WHOLE] * (len(attended) + 1),
            out_specs=WHOLE,
            compiler_params=grant(8),
            cost_estimate=cost(2 * height * depth * cols, depth * cols * 2),
        )(*attended, weights[offset])

    def exchange(block, bit):
        return lax.ppermute(block, "head", [(i, i ^ bit) for i in range(n_head)])

    def halve(blocks):
        bit = 1
        while bit < half:
            for o in sorted(blocks, reverse=True):
                if o & bit:
                    got = exchange(blocks.pop(o), bit)
                    blocks[o ^ bit] = (blocks[o ^ bit].astype(F32) + got.astype(F32)).astype(BF16)
            bit *= 2
        return blocks.popitem()[1]

    attended, crossed = [], []
    for c in range(CHUNKS):
        att, part = attend(c * rows, far)
        blocks = {o: project([att], o) for o in range(n_head - 2, half - 1, -1)}
        blocks[n_head - 1] = part
        total = halve(blocks)
        far, total, att = lax.optimization_barrier((far, total, att))
        attended.append(att)
        crossed.append(exchange(total, half))
    *attended, _ = lax.optimization_barrier((*attended, total))
    near = halve({o: project(attended, o) for o in range(half - 1, -1, -1)})
    return (near.astype(F32) + jnp.concatenate(crossed, axis=0).astype(F32)).astype(BF16)


def solution(mesh):
    placed = (
        P(("groups", "ctx"), "head"),
        P(("groups", "ctx"), "head"),
        P(("groups", "ctx"), "head"),
        P(("groups", "ctx"), None),
        P("groups"),
        P("head", None),
    )
    body = functools.partial(local, n_ctx=mesh.shape["ctx"], n_head=mesh.shape["head"])
    return jax.shard_map(
        body, mesh=mesh, in_specs=placed, out_specs=P(("groups", "ctx"), "head"), check_vma=False
    )
```

time: 41.9 us -> 39.8 us (0.950)
  the two profiles are of different devices: /device:TPU:16 before, /device:TPU:0 now
where the time goes in v3:
time: 39.8 us; the launch traced here: 39.6 us
  waiting for transfers between devices  14.2 us (36%)
  starting transfers between devices  12.2 us (31%)
  Pallas kernels  11 us (28%)
  other arithmetic  1.35 us (3%)
  between operations  0.86 us (2%)
    ppermute x5, waiting for transfers between devices, exchange(): return lax.ppermute(block, 'head', [(i, i ^ bit) for i in range(n_head)])  13.5 us
    ppermute x3, starting transfers between devices, context_rows(): near = [lax.ppermute(message, 'ctx', [(0, shift)]) for shift in range(1, n)]  8.33 us
    pallas_call x1, Pallas kernels, layer(): pl.pallas_call(local_kernel, out_shape=[jax.ShapeDtypeStruct((tokens, mod...  4.24 us
    pallas_call x2, Pallas kernels, attend(): pl.pallas_call(functools.partial(remote_kernel, start), out_shape=[jax.Sh...  3.13 us
    ppermute x5, starting transfers between devices, exchange(): return lax.ppermute(block, 'head', [(i, i ^ bit) for i in range(n_head)])  2.49 us
    pallas_call x4, Pallas kernels, project(): pl.pallas_call(multiply, out_shape=jax.ShapeDtypeStruct((height, cols), B...  2.35 us
    ppermute x2, starting transfers between devices, context_rows(): other = lax.ppermute(kept, 'ctx', rest)  1.33 us
    pallas_call x1, Pallas kernels, layer(): pl.pallas_call(prepare_kernel, out_shape=[jax.ShapeDtypeStruct((ANCHOR +...  1.28 us
  transfers between devices with their start and end apart: 10, of which 5 were waited for; matrix products, arithmetic and copies ran while one was open for 0% of the time, Pallas kernels for 15%

profile of v3, /device:TPU:0, one launch (start us, length us, event | category | flops | bytes accessed | tf_op | source)
XLA Modules:
  0.0 39.6 jit_solution(7399628900994055801)
XLA Ops:
  0.0 1.3 %shard_map.64 = (bf16[160,512]{1,0:T(8,128)(2,1)S(1)}, bf16[256,256]{1,0:T(8,128)(2,1)S(1)}, bf16[256,256]{1,0:T(8,128)(2,1)S(1)}) custom-call(s32[1,32]{1,0:T(1,128)} %pos_hbm.1, bf16[256,256]{1,0:T(8,128)(2,1)} %k_hbm.1, bf16[256,256]{1,0:T(8,128)(2,1)} %v_hbm.1), custom_call_target="tpu_custom_call" | custom-call | flops 8388608 | bytes 262144 | tf_op jit(solution)/shard_map/pallas_call | solution.py:187
  1.3 5.0 %collective-permute-start.2 = (bf16[160,512]{1,0:T(8,128)(2,1)S(1)}, bf16[160,512]{1,0:T(8,128)(2,1)S(1)}, u32[]{:S(2)}, u32[]{:S(2)}) collective-permute-start(bf16[160,512]{1,0:T(8,128)(2,1)S(1)} %get-tuple-element.27), channel_id=1, source_target_pairs={{0,4},{1,5},{2,6},{3,7},{16,20},{17,21},{18,22},{19,23}} | collective-permute-start | bytes 491528 | tf_op jit(solution)/shard_map/ppermute | solution.py:154
  6.3 1.7 %collective-permute-start.1 = (bf16[160,512]{1,0:T(8,128)(2,1)S(1)}, bf16[160,512]{1,0:T(8,128)(2,1)S(1)}, u32[]{:S(2)}, u32[]{:S(2)}) collective-permute-start(bf16[160,512]{1,0:T(8,128)(2,1)S(1)} %get-tuple-element.27), channel_id=1, source_target_pairs={{0,8},{1,9},{2,10},{3,11},{16,24},{17,25},{18,26},{19,27}} | collective-permute-start | bytes 491528 | tf_op jit(solution)/shard_map/ppermute | solution.py:154
  8.0 1.7 %collective-permute-start = (bf16[160,512]{1,0:T(8,128)(2,1)S(1)}, bf16[160,512]{1,0:T(8,128)(2,1)S(1)}, u32[]{:S(2)}, u32[]{:S(2)}) collective-permute-start(bf16[160,512]{1,0:T(8,128)(2,1)S(1)} %get-tuple-element.27), channel_id=1, source_target_pairs={{0,12},{1,13},{2,14},{3,15},{16,28},{17,29},{18,30},{19,31}} | collective-permute-start | bytes 491528 | tf_op jit(solution)/shard_map/ppermute | solution.py:154
  9.7 0.7 %collective-permute-start.3 = (bf16[32,512]{1,0:T(8,128)(2,1)S(1)}, bf16[32,512]{1,0:T(8,128)(2,1)S(1)}, u32[]{:S(2)}, u32[]{:S(2)}) collective-permute-start(bf16[32,512]{1,0:T(8,128)(2,1)S(1)} %slice.25), channel_id=1, source_target_pairs={{4,8},{8,12},{5,9},{9,13},{6,10},{10,14},{7,11},{11,15},{20,24},{2... | collective-permute-start | bytes 98312 | tf_op jit(solution)/shard_map/ppermute | solution.py:162
  10.3 0.7 %collective-permute-start.4 = (bf16[32,512]{1,0:T(8,128)(2,1)S(1)}, bf16[32,512]{1,0:T(8,128)(2,1)S(1)}, u32[]{:S(2)}, u32[]{:S(2)}) collective-permute-start(bf16[32,512]{1,0:T(8,128)(2,1)S(1)} %slice.25), channel_id=1, source_target_pairs={{4,12},{5,13},{6,14},{7,15},{20,28},{21,29},{22,30},{23,31}} | collective-permute-start | bytes 98312 | tf_op jit(solution)/shard_map/ppermute | solution.py:162
  11.7 0.1 pad_add_fusion.info_ref
  11.7 4.2 %shard_map.65 = (f32[256,1024]{1,0:T(8,128)S(1)}, f32[256,1024]{1,0:T(8,128)S(1)}, f32[256,1024]{1,0:T(8,128)S(1)}, bf16[256,1024]{1,0:T(8,128)(2,1)S(1)}, bf16[...) custom-call(s32[3]{0:T(128)S(1)} %pad_add_fusion.info_ref, ...), custom_call_target="tpu_custom_call" | custom-call | flops 268435456 | bytes 1572864 | tf_op jit(solution)/shard_map/pallas_call | solution.py:202
  16.0 0.0 collective-permute-done.2
  16.0 0.0 collective-permute-done.1
  16.0 0.8 %collective-permute-done = bf16[160,512]{1,0:T(8,128)(2,1)S(1)} collective-permute-done((bf16[160,512]{1,0:T(8,128)(2,1)S(1)}, bf16[160,512]{1,0:T(8,128)(2,1)S(1)}, u32[]{:S(2)}, u32[]{:S(2)}) %collective-permute-start) | collective-permute-done | bytes 163872 | tf_op jit(solution)/shard_map/ppermute | solution.py:154
  16.8 0.1 fusion.2
  16.8 0.0 collective-permute-done.3
  16.8 0.0 collective-permute-done.4
  16.9 1.6 %shard_map.66 = (bf16[128,1024]{1,0:T(8,128)(2,1)S(1)}, bf16[128,1024]{1,0:T(8,128)(2,1)S(1)}) custom-call(s32[3]{0:T(128)S(1)} %pad_add_fusion.info_ref, bf16[256,1024]{1,0:T(8,128)(2,1)S(1)} %get-tuple-element.30.q_ref, bf16[256,512]{1,0:T(8,128)(2,1)S(1)} %broadcast_dynamic-update-slice_fusion.far_ref, f32[256,1024]{1,0:T(8,128)S(1)} %get-tuple-element.31.num_ref, ...), custom_call_target="tpu_custom_call" | custom-call | flops 402653184 | bytes 2097152 | tf_op jit(solution)/shard_map/pallas_call | solution.py:227
  18.5 0.1 collective-permute-start.5
  18.6 0.4 %shard_map.67 = bf16[128,1024]{1,0:T(8,128)(2,1)S(1)} custom-call(bf16[128,1024]{1,0:T(8,128)(2,1)S(1)} %get-tuple-element.44.refs_0_, bf16[1024,1024]{1,0:T(8,128)(2,1)S(1)} %get-tuple-element.36.refs_1_), custom_call_target="tpu_custom_call" | custom-call | flops 268435456 | bytes 2097152 | tf_op jit(solution)/shard_map/pallas_call | solution.py:245
  19.0 1.1 %collective-permute-done.5 = bf16[128,1024]{1,0:T(8,128)(2,1)S(1)} collective-permute-done((bf16[128,1024]{1,0:T(8,128)(2,1)S(1)}, bf16[128,1024]{1,0:T(8,128)(2,1)S(1)}, u32[]{:S(2)}, u32[]{:S(2)}) %collective-permute-start.5) | collective-permute-done | bytes 262176 | tf_op jit(solution)/shard_map/ppermute | solution.py:255
  20.1 0.1 add_convert_fusion.3
  20.1 1.6 %shard_map.68 = (bf16[128,1024]{1,0:T(8,128)(2,1)S(1)}, bf16[128,1024]{1,0:T(8,128)(2,1)S(1)}) custom-call(s32[3]{0:T(128)S(1)} %pad_add_fusion.info_ref, bf16[256,1024]{1,0:T(8,128)(2,1)S(1)} %get-tuple-element.30.q_ref, bf16[256,512]{1,0:T(8,128)(2,1)S(1)} %broadcast_dynamic-update-slice_fusion.far_ref, f32[256,1024]{1,0:T(8,128)S(1)} %get-tuple-element.31.num_ref, ...), custom_call_target="tpu_custom_call" | custom-call | flops 402653184 | bytes 2097152 | tf_op jit(solution)/shard_map/pallas_call | solution.py:227
  21.7 0.2 collective-permute-start.6
  21.9 0.4 %shard_map.69 = bf16[128,1024]{1,0:T(8,128)(2,1)S(1)} custom-call(bf16[128,1024]{1,0:T(8,128)(2,1)S(1)} %get-tuple-element.45.refs_0_.refs_1_, bf16[1024,1024]{1,0:T(8,128)(2,1)S(1)} %get-tuple-element.36.refs_1_), custom_call_target="tpu_custom_call" | custom-call | flops 268435456 | bytes 2097152 | tf_op jit(solution)/shard_map/pallas_call | solution.py:245
  22.4 0.9 %collective-permute-done.6 = bf16[128,1024]{1,0:T(8,128)(2,1)S(1)} collective-permute-done((bf16[128,1024]{1,0:T(8,128)(2,1)S(1)}, bf16[128,1024]{1,0:T(8,128)(2,1)S(1)}, u32[]{:S(2)}, u32[]{:S(2)}) %collective-permute-start.6) | collective-permute-done | bytes 262176 | tf_op jit(solution)/shard_map/ppermute | solution.py:255
  23.3 0.1 add_convert_fusion.2
  23.4 0.7 %shard_map.71 = bf16[256,1024]{1,0:T(8,128)(2,1)S(1)} custom-call(bf16[128,1024]{1,0:T(8,128)(2,1)S(1)} %get-tuple-element.44.refs_0_, bf16[128,1024]{1,0:T(8,128)(2,1)S(1)} %get-tuple-element.45.refs_0_.refs_1_, bf16[1024,1024]{1,0:T(8,128)(2,1)S(1)} %get-tuple-element.47.refs_2_), custom_call_target="tpu_custom_call" | custom-call | flops 536870912 | bytes 2097152 | tf_op jit(solution)/shard_map/pallas_call | solution.py:245
  24.1 0.2 collective-permute-start.7
  24.3 1.5 %collective-permute-start.8 = (bf16[128,1024]{1,0:T(8,128)(2,1)S(1)}, bf16[128,1024]{1,0:T(8,128)(2,1)S(1)}, u32[]{:S(2)}, u32[]{:S(2)}) collective-permute-start(bf16[128,1024]{1,0:T(8,128)(2,1)S(1)} %add_convert_fusion.3), channel_id=1, source_target_pairs={{0,2},{1,3},{2,0},{3,1},{4,6},{5,7},{6,4},{7,5},{8,10},{9,11},{10,... | collective-permute-start | bytes 786440 | tf_op jit(solution)/shard_map/ppermute | solution.py:255
  25.8 0.5 %collective-permute-start.9 = (bf16[128,1024]{1,0:T(8,128)(2,1)S(1)}, bf16[128,1024]{1,0:T(8,128)(2,1)S(1)}, u32[]{:S(2)}, u32[]{:S(2)}) collective-permute-start(bf16[128,1024]{1,0:T(8,128)(2,1)S(1)} %add_convert_fusion.2), channel_id=1, source_target_pairs={{0,2},{1,3},{2,0},{3,1},{4,6},{5,7},{6,4},{7,5},{8,10},{9,11},{10,... | collective-permute-start | bytes 786440 | tf_op jit(solution)/shard_map/ppermute | solution.py:255
  26.4 0.7 %shard_map.70 = bf16[256,1024]{1,0:T(8,128)(2,1)S(1)} custom-call(bf16[128,1024]{1,0:T(8,128)(2,1)S(1)} %get-tuple-element.44.refs_0_, bf16[128,1024]{1,0:T(8,128)(2,1)S(1)} %get-tuple-element.45.refs_0_.refs_1_, bf16[1024,1024]{1,0:T(8,128)(2,1)S(1)} %get-tuple-element.46.refs_2_), custom_call_target="tpu_custom_call" | custom-call | flops 536870912 | bytes 2097152 | tf_op jit(solution)/shard_map/pallas_call | solution.py:245
  27.1 6.4 %collective-permute-done.8 = bf16[128,1024]{1,0:T(8,128)(2,1)S(1)} collective-permute-done((bf16[128,1024]{1,0:T(8,128)(2,1)S(1)}, bf16[128,1024]{1,0:T(8,128)(2,1)S(1)}, u32[]{:S(2)}, u32[]{:S(2)}) %collective-permute-start.8) | collective-permute-done | bytes 262176 | tf_op jit(solution)/shard_map/ppermute | solution.py:255
  33.5 5.0 %collective-permute-done.9 = bf16[128,1024]{1,0:T(8,128)(2,1)S(1)} collective-permute-done((bf16[128,1024]{1,0:T(8,128)(2,1)S(1)}, bf16[128,1024]{1,0:T(8,128)(2,1)S(1)}, u32[]{:S(2)}, u32[]{:S(2)}) %collective-permute-start.9) | collective-permute-done | bytes 262176 | tf_op jit(solution)/shard_map/ppermute | solution.py:255
  38.5 0.0 collective-permute-done.7
  38.5 1.1 %add_convert_fusion = bf16[256,1024]{1,0:T(8,128)(2,1)} fusion(bf16[256,1024]{1,0:T(8,128)(2,1)S(1)} %collective-permute-done.7, bf16[256,1024]{1,0:T(8,128)(2,1)S(1)} %shard_map.70, bf16[128,1024]{1,0:T(8,128)(2,1)S(1)} %collective-permute-done.9, bf16[128,1024]{1,0:T(8,128)(2,1)S(1)} %collective-permute-done.8), kind=kLoop, calls=%fused_computation | loop fusion | flops 2883584 | bytes 2097152 | tf_op jit(solution)/shard_map/convert_element_type | solution.py:278
  (5 shorter events, 0.0 us)
Async XLA Ops:
  1.3 14.7 %collective-permute-start.2 = (bf16[160,512]{1,0:T(8,128)(2,1)S(1)}, bf16[160,512]{1,0:T(8,128)(2,1)S(1)}, u32[]{:S(2)}, u32[]{:S(2)}) collective-permute-start(bf16[160,512]{1,0:T(8,128)(2,1)S(1)} %get-tuple-element.27), channel_id=1, source_target_pairs={{0,4},{1,5},{2,6},{3,7},{16,20},{17,21},{18,22},{19,23}} | collective-permute-start | bytes 491528 | tf_op jit(solution)/shard_map/ppermute | solution.py:154
  6.3 9.7 %collective-permute-start.1 = (bf16[160,512]{1,0:T(8,128)(2,1)S(1)}, bf16[160,512]{1,0:T(8,128)(2,1)S(1)}, u32[]{:S(2)}, u32[]{:S(2)}) collective-permute-start(bf16[160,512]{1,0:T(8,128)(2,1)S(1)} %get-tuple-element.27), channel_id=1, source_target_pairs={{0,8},{1,9},{2,10},{3,11},{16,24},{17,25},{18,26},{19,27}} | collective-permute-start | bytes 491528 | tf_op jit(solution)/shard_map/ppermute | solution.py:154
  8.0 8.8 %collective-permute-start = (bf16[160,512]{1,0:T(8,128)(2,1)S(1)}, bf16[160,512]{1,0:T(8,128)(2,1)S(1)}, u32[]{:S(2)}, u32[]{:S(2)}) collective-permute-start(bf16[160,512]{1,0:T(8,128)(2,1)S(1)} %get-tuple-element.27), channel_id=1, source_target_pairs={{0,12},{1,13},{2,14},{3,15},{16,28},{17,29},{18,30},{19,31}} | collective-permute-start | bytes 491528 | tf_op jit(solution)/shard_map/ppermute | solution.py:154
  9.7 7.2 %collective-permute-start.3 = (bf16[32,512]{1,0:T(8,128)(2,1)S(1)}, bf16[32,512]{1,0:T(8,128)(2,1)S(1)}, u32[]{:S(2)}, u32[]{:S(2)}) collective-permute-start(bf16[32,512]{1,0:T(8,128)(2,1)S(1)} %slice.25), channel_id=1, source_target_pairs={{4,8},{8,12},{5,9},{9,13},{6,10},{10,14},{7,11},{11,15},{20,24},{2... | collective-permute-start | bytes 98312 | tf_op jit(solution)/shard_map/ppermute | solution.py:162
  10.3 6.5 %collective-permute-start.4 = (bf16[32,512]{1,0:T(8,128)(2,1)S(1)}, bf16[32,512]{1,0:T(8,128)(2,1)S(1)}, u32[]{:S(2)}, u32[]{:S(2)}) collective-permute-start(bf16[32,512]{1,0:T(8,128)(2,1)S(1)} %slice.25), channel_id=1, source_target_pairs={{4,12},{5,13},{6,14},{7,15},{20,28},{21,29},{22,30},{23,31}} | collective-permute-start | bytes 98312 | tf_op jit(solution)/shard_map/ppermute | solution.py:162
  18.5 1.6 %collective-permute-start.5 = (bf16[128,1024]{1,0:T(8,128)(2,1)S(1)}, bf16[128,1024]{1,0:T(8,128)(2,1)S(1)}, u32[]{:S(2)}, u32[]{:S(2)}) collective-permute-start(bf16[128,1024]{1,0:T(8,128)(2,1)S(1)} %get-tuple-element.37), channel_id=1, source_target_pairs={{0,1},{1,0},{2,3},{3,2},{4,5},{5,4},{6,7},{7,6},{8,9},{9,8},{10,11... | collective-permute-start | bytes 786440 | tf_op jit(solution)/shard_map/ppermute | solution.py:255
  21.7 1.6 %collective-permute-start.6 = (bf16[128,1024]{1,0:T(8,128)(2,1)S(1)}, bf16[128,1024]{1,0:T(8,128)(2,1)S(1)}, u32[]{:S(2)}, u32[]{:S(2)}) collective-permute-start(bf16[128,1024]{1,0:T(8,128)(2,1)S(1)} %get-tuple-element.41), channel_id=1, source_target_pairs={{0,1},{1,0},{2,3},{3,2},{4,5},{5,4},{6,7},{7,6},{8,9},{9,8},{10,11... | collective-permute-start | bytes 786440 | tf_op jit(solution)/shard_map/ppermute | solution.py:255
  24.1 14.4 %collective-permute-start.7 = (bf16[256,1024]{1,0:T(8,128)(2,1)S(1)}, bf16[256,1024]{1,0:T(8,128)(2,1)S(1)}, u32[]{:S(2)}, u32[]{:S(2)}) collective-permute-start(bf16[256,1024]{1,0:T(8,128)(2,1)S(1)} %shard_map.71), channel_id=1, source_target_pairs={{0,1},{1,0},{2,3},{3,2},{4,5},{5,4},{6,7},{7,6},{8,9},{9,8},{10,11... | collective-permute-start | bytes 1572872 | tf_op jit(solution)/shard_map/ppermute | solution.py:255
  24.3 9.2 %collective-permute-start.8 = (bf16[128,1024]{1,0:T(8,128)(2,1)S(1)}, bf16[128,1024]{1,0:T(8,128)(2,1)S(1)}, u32[]{:S(2)}, u32[]{:S(2)}) collective-permute-start(bf16[128,1024]{1,0:T(8,128)(2,1)S(1)} %add_convert_fusion.3), channel_id=1, source_target_pairs={{0,2},{1,3},{2,0},{3,1},{4,6},{5,7},{6,4},{7,5},{8,10},{9,11},{10,... | collective-permute-start | bytes 786440 | tf_op jit(solution)/shard_map/ppermute | solution.py:255
  25.8 12.7 %collective-permute-start.9 = (bf16[128,1024]{1,0:T(8,128)(2,1)S(1)}, bf16[128,1024]{1,0:T(8,128)(2,1)S(1)}, u32[]{:S(2)}, u32[]{:S(2)}) collective-permute-start(bf16[128,1024]{1,0:T(8,128)(2,1)S(1)} %add_convert_fusion.2), channel_id=1, source_target_pairs={{0,2},{1,3},{2,0},{3,1},{4,6},{5,7},{6,4},{7,5},{8,10},{9,11},{10,... | collective-permute-start | bytes 786440 | tf_op jit(solution)/shard_map/ppermute | solution.py:255
